TPU v7x, 32 devices: a 4x4x1 block of a 4x4x8 slice. The times are simulated.
32 devices in a mesh: dp: 1 (over z), cp: 32 (over y, x, core).
Axes of the slice: x: 4, y: 4, z: 1, core: 2. Of those that a mesh axis runs over, the one named last changes fastest.
The devices are a block of a 4x4x8 slice.
Arguments:
- x_norm: bfloat16 [4096, 2048], P(('dp', 'cp'))
- y_grad: bfloat16 [4096, 2048], P(('dp', 'cp'))
- w_q: bfloat16 [2048, 16, 192], replicated
- w_dkv: bfloat16 [2048, 512], replicated
- g_kv: bfloat16 [512], replicated
- w_kr: bfloat16 [2048, 64], replicated
- w_uk: bfloat16 [512, 16, 128], replicated
- w_uv: bfloat16 [512, 16, 128], replicated
- w_o: bfloat16 [16, 128, 2048], replicated
Outputs:
- output 1: bfloat16 [4096, 2048], P(('dp', 'cp'))
- output 2: bfloat16 [4096, 2048], P(('dp', 'cp'))
- output 3: float32 [2048, 16, 192], P('dp')
- output 4: float32 [2048, 512], P('dp')
- output 5: float32 [512], P('dp')
- output 6: float32 [2048, 64], P('dp')
- output 7: float32 [512, 16, 128], P('dp')
- output 8: float32 [512, 16, 128], P('dp')
- output 9: float32 [16, 128, 2048], P('dp')
All inputs are finite; a program needn't handle non-finite values.
Results may differ from a plain program's by a relative error of at most 0.02.
Values are sent between devices in bfloat16 or wider.
A program may use at most 768 MiB of HBM per device.

v0:
```python
import jax
import jax.numpy as jnp
from jax import lax
from jax.sharding import PartitionSpec as P

ROPE_THETA = 10000.0
NORM_EPS = 1e-6


def rope_tables(positions, rope_dim):
    half_dim = rope_dim // 2
    inv_freq = ROPE_THETA ** (-(jnp.arange(half_dim, dtype=jnp.float32) * 2.0 / rope_dim))
    angles = positions.astype(jnp.float32)[:, None] * inv_freq[None, :]
    return jnp.cos(angles), jnp.sin(angles)


def rope_apply(t_in, cos_t, sin_t):
    half_dim = t_in.shape[-1] // 2
    first_half = t_in[..., :half_dim]
    second_half = t_in[..., half_dim:]
    return jnp.concatenate([first_half * cos_t - second_half * sin_t, second_half * cos_t + first_half * sin_t], axis=-1)


def rope_back(g_in, cos_t, sin_t):
    half_dim = g_in.shape[-1] // 2
    first_half = g_in[..., :half_dim]
    second_half = g_in[..., half_dim:]
    return jnp.concatenate([first_half * cos_t + second_half * sin_t, second_half * cos_t - first_half * sin_t], axis=-1)


def project_local(x_loc, w_q, w_dkv, g_kv, w_kr, cos_t, sin_t):
    nope_dim = w_q.shape[2] - w_kr.shape[1]
    q_full = jnp.einsum('td,dhe->the', x_loc, w_q, preferred_element_type=jnp.float32)
    q_nope = q_full[..., :nope_dim].astype(jnp.bfloat16)
    q_rope = rope_apply(q_full[..., nope_dim:], cos_t[:, None, :], sin_t[:, None, :]).astype(jnp.bfloat16)
    c_raw = jnp.dot(x_loc, w_dkv, preferred_element_type=jnp.float32)
    inv_rms = lax.rsqrt(jnp.mean(c_raw * c_raw, axis=-1, keepdims=True) + NORM_EPS)
    c_norm = c_raw * inv_rms
    latent = (c_norm * g_kv.astype(jnp.float32)).astype(jnp.bfloat16)
    k_rope = rope_apply(jnp.dot(x_loc, w_kr, preferred_element_type=jnp.float32), cos_t, sin_t).astype(jnp.bfloat16)
    return q_nope, q_rope, c_norm, inv_rms, latent, k_rope


def project_back(x_loc, w_q, w_dkv, g_kv, w_kr, cos_t, sin_t, dq_nope, dq_rope, d_latent, dk_rope, c_norm, inv_rms):
    dq_full = jnp.concatenate([dq_nope, rope_back(dq_rope, cos_t[:, None, :], sin_t[:, None, :])], axis=-1).astype(jnp.bfloat16)
    d_norm = d_latent * g_kv.astype(jnp.float32)
    gg_kv = jnp.sum(d_latent * c_norm, axis=0)
    dc_raw = (inv_rms * (d_norm - c_norm * jnp.mean(d_norm * c_norm, axis=-1, keepdims=True))).astype(jnp.bfloat16)
    dkr_raw = rope_back(dk_rope, cos_t, sin_t).astype(jnp.bfloat16)
    gw_q = jnp.einsum('td,the->dhe', x_loc, dq_full, preferred_element_type=jnp.float32)
    gw_dkv = jnp.einsum('td,tc->dc', x_loc, dc_raw, preferred_element_type=jnp.float32)
    gw_kr = jnp.einsum('td,tr->dr', x_loc, dkr_raw, preferred_element_type=jnp.float32)
    dx_loc = (jnp.einsum('the,dhe->td', dq_full, w_q, preferred_element_type=jnp.float32) + jnp.einsum('tc,dc->td', dc_raw, w_dkv, preferred_element_type=jnp.float32) + jnp.einsum('tr,dr->td', dkr_raw, w_kr, preferred_element_type=jnp.float32))
    return dx_loc, gw_q, gw_dkv, gg_kv, gw_kr


def key_mask(my_idx, blk_idx, chunk_len):
    q_pos = my_idx * chunk_len + jnp.arange(chunk_len)
    k_pos = blk_idx * chunk_len + jnp.arange(chunk_len)
    return (q_pos[:, None] >= k_pos[None, :])[None]


def block_scores(q_nope, q_rope, k_nope, k_rope, mask_blk, attn_scale):
    scores = (jnp.einsum('qhn,khn->hqk', q_nope, k_nope, preferred_element_type=jnp.float32) + jnp.einsum('qhr,kr->hqk', q_rope, k_rope, preferred_element_type=jnp.float32)) * attn_scale
    return jnp.where(mask_blk, scores, -jnp.inf)


def add_rows(buffer, block, row_start):
    current = lax.dynamic_slice_in_dim(buffer, row_start, block.shape[0], 0)
    return lax.dynamic_update_slice_in_dim(buffer, current + block, row_start, 0)


def attend_forward(q_nope, q_rope, k_nope_all, k_rope_all, v_all, my_idx, attn_scale):
    chunk_len = q_nope.shape[0]
    num_heads = q_nope.shape[1]
    v_dim = v_all.shape[2]

    def fwd_step(blk_idx, loop_state):
        run_max, run_sum, acc_out = loop_state
        blk_start = blk_idx * chunk_len
        k_nope = lax.dynamic_slice_in_dim(k_nope_all, blk_start, chunk_len, 0)
        k_rope = lax.dynamic_slice_in_dim(k_rope_all, blk_start, chunk_len, 0)
        v_blk = lax.dynamic_slice_in_dim(v_all, blk_start, chunk_len, 0)
        scores = block_scores(q_nope, q_rope, k_nope, k_rope, key_mask(my_idx, blk_idx, chunk_len), attn_scale)
        new_max = jnp.maximum(run_max, jnp.max(scores, axis=-1))
        rescale = jnp.exp(run_max - new_max)
        prob = jnp.exp(scores - new_max[..., None])
        run_sum = run_sum * rescale + jnp.sum(prob, axis=-1)
        acc_out = acc_out * rescale[..., None] + jnp.einsum('hqk,khv->hqv', prob.astype(jnp.bfloat16), v_blk, preferred_element_type=jnp.float32)
        return new_max, run_sum, acc_out

    init_state = (jnp.full((num_heads, chunk_len), -jnp.inf, jnp.float32), jnp.zeros((num_heads, chunk_len), jnp.float32), jnp.zeros((num_heads, chunk_len, v_dim), jnp.float32))
    run_max, run_sum, acc_out = lax.fori_loop(0, my_idx + 1, fwd_step, init_state)
    return acc_out / run_sum[..., None], run_max + jnp.log(run_sum)


def attend_backward(q_nope, q_rope, k_nope_all, k_rope_all, v_all, d_out, log_sum, row_dot, my_idx, attn_scale):
    chunk_len = q_nope.shape[0]

    def bwd_step(blk_idx, loop_state):
        dq_nope, dq_rope, dk_nope_all, dk_rope_all, dv_all = loop_state
        blk_start = blk_idx * chunk_len
        k_nope = lax.dynamic_slice_in_dim(k_nope_all, blk_start, chunk_len, 0)
        k_rope = lax.dynamic_slice_in_dim(k_rope_all, blk_start, chunk_len, 0)
        v_blk = lax.dynamic_slice_in_dim(v_all, blk_start, chunk_len, 0)
        scores = block_scores(q_nope, q_rope, k_nope, k_rope, key_mask(my_idx, blk_idx, chunk_len), attn_scale)
        prob = jnp.exp(scores - log_sum[..., None])
        dv_blk = jnp.einsum('hqk,hqv->khv', prob.astype(jnp.bfloat16), d_out, preferred_element_type=jnp.float32)
        d_prob = jnp.einsum('hqv,khv->hqk', d_out, v_blk, preferred_element_type=jnp.float32)
        d_score = (prob * (d_prob - row_dot[..., None]) * attn_scale).astype(jnp.bfloat16)
        dq_nope = dq_nope + jnp.einsum('hqk,khn->qhn', d_score, k_nope, preferred_element_type=jnp.float32)
        dq_rope = dq_rope + jnp.einsum('hqk,kr->qhr', d_score, k_rope, preferred_element_type=jnp.float32)
        dk_blk = jnp.einsum('hqk,qhn->khn', d_score, q_nope, preferred_element_type=jnp.float32)
        dkr_blk = jnp.einsum('hqk,qhr->kr', d_score, q_rope, preferred_element_type=jnp.float32)
        dk_nope_all = add_rows(dk_nope_all, dk_blk, blk_start)
        dk_rope_all = add_rows(dk_rope_all, dkr_blk, blk_start)
        dv_all = add_rows(dv_all, dv_blk, blk_start)
        return dq_nope, dq_rope, dk_nope_all, dk_rope_all, dv_all

    init_state = (jnp.zeros(q_nope.shape, jnp.float32), jnp.zeros(q_rope.shape, jnp.float32), jnp.zeros(k_nope_all.shape, jnp.float32), jnp.zeros(k_rope_all.shape, jnp.float32), jnp.zeros(v_all.shape, jnp.float32))
    return lax.fori_loop(0, my_idx + 1, bwd_step, init_state)


def solution(mesh):
    row_spec = P(('dp', 'cp'), None)
    in_specs = (row_spec, row_spec, P(), P(), P(), P(), P(), P(), P())
    out_specs = (row_spec, row_spec, P('dp', None, None), P('dp', None), P('dp'), P('dp', None), P('dp', None, None), P('dp', None, None), P('dp', None, None))

    def device_fn(x_loc, gy_loc, w_q, w_dkv, g_kv, w_kr, w_uk, w_uv, w_o):
        chunk_len = x_loc.shape[0]
        attn_scale = w_q.shape[2] ** -0.5
        my_idx = lax.axis_index('cp')
        cos_t, sin_t = rope_tables(my_idx * chunk_len + jnp.arange(chunk_len), w_kr.shape[1])
        q_nope, q_rope, c_norm, inv_rms, latent, k_rope = project_local(x_loc, w_q, w_dkv, g_kv, w_kr, cos_t, sin_t)
        k_nope = jnp.einsum('tc,chn->thn', latent, w_uk, preferred_element_type=jnp.float32).astype(jnp.bfloat16)
        v_loc = jnp.einsum('tc,chv->thv', latent, w_uv, preferred_element_type=jnp.float32).astype(jnp.bfloat16)
        k_nope_all = lax.all_gather(k_nope, 'cp', axis=0, tiled=True)
        k_rope_all = lax.all_gather(k_rope, 'cp', axis=0, tiled=True)
        v_all = lax.all_gather(v_loc, 'cp', axis=0, tiled=True)
        attn_out, log_sum = attend_forward(q_nope, q_rope, k_nope_all, k_rope_all, v_all, my_idx, attn_scale)
        attn_bf16 = attn_out.astype(jnp.bfloat16)
        y_loc = jnp.einsum('hqv,hvd->qd', attn_bf16, w_o, preferred_element_type=jnp.float32).astype(jnp.bfloat16)
        d_out = jnp.einsum('qd,hvd->hqv', gy_loc, w_o, preferred_element_type=jnp.float32).astype(jnp.bfloat16)
        gw_o = jnp.einsum('hqv,qd->hvd', attn_bf16, gy_loc, preferred_element_type=jnp.float32)
        row_dot = jnp.sum(d_out.astype(jnp.float32) * attn_out, axis=-1)
        dq_nope, dq_rope, dk_nope_all, dk_rope_all, dv_all = attend_backward(q_nope, q_rope, k_nope_all, k_rope_all, v_all, d_out, log_sum, row_dot, my_idx, attn_scale)
        dk_nope = lax.psum_scatter(dk_nope_all, 'cp', scatter_dimension=0, tiled=True).astype(jnp.bfloat16)
        dk_rope = lax.psum_scatter(dk_rope_all, 'cp', scatter_dimension=0, tiled=True)
        dv_loc = lax.psum_scatter(dv_all, 'cp', scatter_dimension=0, tiled=True).astype(jnp.bfloat16)
        gw_uk = jnp.einsum('tc,thn->chn', latent, dk_nope, preferred_element_type=jnp.float32)
        gw_uv = jnp.einsum('tc,thv->chv', latent, dv_loc, preferred_element_type=jnp.float32)
        d_latent = jnp.einsum('thn,chn->tc', dk_nope, w_uk, preferred_element_type=jnp.float32) + jnp.einsum('thv,chv->tc', dv_loc, w_uv, preferred_element_type=jnp.float32)
        dx_loc, gw_q, gw_dkv, gg_kv, gw_kr = project_back(x_loc, w_q, w_dkv, g_kv, w_kr, cos_t, sin_t, dq_nope, dq_rope, d_latent, dk_rope, c_norm, inv_rms)
        weight_grads = lax.psum((gw_q, gw_dkv, gg_kv, gw_kr, gw_uk, gw_uv, gw_o), 'cp')
        return (y_loc, dx_loc.astype(jnp.bfloat16)) + tuple(weight_grads)

    return jax.shard_map(device_fn, mesh=mesh, in_specs=in_specs, out_specs=out_specs, check_vma=False)
```

profile of v0, /device:TPU:97, one launch (start us, length us, event | category | flops | bytes accessed | tf_op | source)
XLA Modules:
  0.0 1667.9 jit_solution(16964189140478783750)
XLA Ops:
  15.2 6.5 fusion.105
  26.7 36.4 %all_gather.10 = bf16[4096,64]{0,1:T(8,128)(2,1)S(1)} all-gather(bf16[128,64]{0,1:T(8,128)(2,1)S(1)} %pad_maximum_fusion.4), channel_id=1, replica_groups=mesh['dp'=1,'cp'=32] {'cp'}, dimensions={0}, use_global_device_ids=true | all-gather | bytes 540672 | tf_op jit(solution)/shard_map/all_gather | solution.py:138
  63.1 24.4 %all-gather.3.cloned.1.call-done = bf16[4096,16,128]{2,0,1:T(8,128)(2,1)} async-done(((bf16[128,16,128]{2,0,1:T(8,128)(2,1)}), bf16[4096,16,128]{2,0,1:T(8,128)(2,1)}) %all-gather.3.cloned.1.call-update) | async-done | bytes 16777232 | tf_op jit(solution)/shard_map/all_gather | solution.py:137
  87.5 69.4 %all-gather.5.cloned.1.call-done = bf16[4096,16,128]{2,0,1:T(8,128)(2,1)} async-done(((bf16[128,16,128]{2,0,1:T(8,128)(2,1)}), bf16[4096,16,128]{2,0,1:T(8,128)(2,1)}) %all-gather.5.cloned.1.call-update) | async-done | bytes 16777232 | tf_op jit(solution)/shard_map/all_gather | solution.py:139
  158.0 9.9 while.36
  170.6 6.9 multiply_reduce_fusion
  178.9 11.0 broadcast.154
  189.9 11.0 broadcast.154.clone
  203.9 31.3 %while.37 = (s32[]{:T(128)}, f32[128,16,128]{0,2,1:T(8,128)}, f32[128,16,64]{0,2,1:T(8,128)}, f32[4096,16,128]{2,0,1:T(8,128)}, f32[4096,64]{0,1:T(8,128)}, /*in...) while((s32[]{:T(128)}, f32[128,16,128]{0,2,1:T(8,128)}, ...), condition=%wide.region_7.8_spmd, body=%wide.region_6.7_spmd.sunk | while | flops 439509248 | bytes 19548428 | solution.py:121
  239.5 9.8 fusion.71
  249.3 10.8 convolution_bitcast_fusion.9
  260.1 660.9 %reduce-scatter.8.cloned.1.call-done = f32[128,64]{0,1:T(8,128)} async-done(((f32[4096,64]{0,1:T(8,128)}), f32[128,64]{0,1:T(8,128)}) %reduce-scatter.8.cloned.1.call-update) | async-done | bytes 32784 | tf_op jit(solution)/shard_map/reduce_scatter | solution.py:148
  922.9 158.8 %reduce-scatter.4.cloned.1.call-done = f32[128,16,128]{2,0,1:T(8,128)} async-done(((f32[4096,16,128]{2,0,1:T(8,128)}), f32[128,16,128]{2,0,1:T(8,128)}) %reduce-scatter.4.cloned.1.call-update) | async-done | bytes 1048592 | tf_op jit(solution)/shard_map/reduce_scatter | solution.py:147
  1081.7 3.5 fusion.61
  1085.1 156.4 %reduce-scatter.6.cloned.1.call-done = f32[128,16,128]{2,0,1:T(8,128)} async-done(((f32[4096,16,128]{2,0,1:T(8,128)}), f32[128,16,128]{2,0,1:T(8,128)}) %reduce-scatter.6.cloned.1.call-update) | async-done | bytes 1048592 | tf_op jit(solution)/shard_map/reduce_scatter | solution.py:149
  1254.7 5.5 fusion.44
  1260.3 6.4 convolution_bitcast_fusion.12
  1266.7 47.0 %psum.51 = f32[512]{0:T(512)} all-reduce(f32[512]{0:T(512)} %get-tuple-element.374), channel_id=1, replica_groups=mesh['dp'=1,'cp'=32] {'cp'}, use_global_device_ids=true, to_apply=%region_15.16 | all-reduce | flops 512 | bytes 4096 | tf_op jit(solution)/shard_map/psum | solution.py:154
  1317.2 300.6 %all-reduce.3.cloned.1.call-done = (f32[2048,16,192]{0,2,1:T(8,128)}, f32[2048,512]{0,1:T(8,128)}, f32[2048,64]{0,1:T(8,128)}, f32[512,16,128]{2,0,1:T(8,128)}, ...) async-done(((f32[2048,16,192]{0,2,1:T(8,128)}, f32[2048,512]{0,1:T(8,128)}, f32[2048,64]{0,1:T(8,128)}, f32[512,16,128]{2,0,1:T(8,128)}, f32[512,16,128]{2,0,1:T(8,128)}, ...) | async-done | bytes 55050256 | tf_op jit(solution)/shard_map/psum | solution.py:154
  1617.8 5.3 copy.34
  1623.2 6.8 copy.35
  1630.0 4.4 copy.36
  1634.4 19.7 %copy.106 = f32[2048,16,192]{0,2,1:T(8,128)} copy(f32[2048,16,192]{0,2,1:T(8,128)} %get-tuple-element.750) | data formatting | bytes 50331648
  1654.9 6.2 copy.108
  (150 shorter events, 85.5 us)
Async XLA Ops:
  7.2 80.3 %all-gather.3.cloned.1.call-start = ((), (), s32[]{:S(2)}) async-start(), calls=%async_computation.3 | async-start | bytes 17301504 | tf_op jit(solution)/shard_map/all_gather | solution.py:137
  9.7 1231.8 %copy-start.24 = (f32[128]{0:T(128)}, f32[128]{0:T(128)S(1)}, u32[]{:S(2)}) copy-start(f32[128]{0:T(128)S(1)} %add_rsqrt_fusion) | copy-start | bytes 1540
  10.5 1231.0 %copy-start.23 = (f32[512]{0:T(512)}, f32[512]{0:T(512)S(1)}, u32[]{:S(2)}) copy-start(f32[512]{0:T(512)S(1)} %convert_element_type.67) | copy-start | bytes 6148
  10.6 11.1 copy-start.14
  13.6 143.2 %all-gather.5.cloned.1.call-start = ((), (), s32[]{:S(2)}) async-start(), calls=%async_computation.4 | async-start | bytes 17301504 | tf_op jit(solution)/shard_map/all_gather | solution.py:139
  15.1 905.9 %reduce-scatter.8.cloned.1.call-start = ((), (), s32[]{:S(2)}) async-start(), calls=%async_computation.7 | async-start | bytes 1081344 | tf_op jit(solution)/shard_map/reduce_scatter | solution.py:148
  15.2 9.9 copy-start.17
  167.9 9.7 copy-start.16
  235.3 846.4 %reduce-scatter.4.cloned.1.call-start = ((), (), s32[]{:S(2)}) async-start(), calls=%async_computation.5 | async-start | bytes 34603008 | tf_op jit(solution)/shard_map/reduce_scatter | solution.py:147
  235.9 1005.6 %reduce-scatter.6.cloned.1.call-start = ((), (), s32[]{:S(2)}) async-start(), calls=%async_computation.6 | async-start | bytes 34603008 | tf_op jit(solution)/shard_map/reduce_scatter | solution.py:149
  236.6 1381.3 %all-reduce.3.cloned.1.call-start = ((), (), s32[]{:S(2)}) async-start(), calls=%async_computation.8 | async-start | bytes 110100480 | tf_op jit(solution)/shard_map/psum | solution.py:154
  238.2 11.1 copy-start.6
  239.5 9.8 copy-start.4
  260.1 981.5 %copy-start.10 = (f32[128,512]{1,0:T(8,128)S(1)}, f32[128,512]{1,0:T(8,128)}, u32[]{:S(2)}) copy-start(f32[128,512]{1,0:T(8,128)} %copy-done.9) | copy-start | bytes 786436
  921.8 322.6 %copy-start.21 = (bf16[128,32]{0,1:T(8,128)(2,1)}, bf16[128,32]{0,1:T(8,128)(2,1)S(1)}, u32[]{:S(2)}) copy-start(bf16[128,32]{0,1:T(8,128)(2,1)S(1)} %get-tuple-element.449) | copy-start | bytes 24580
  1085.1 162.9 %copy-start.15 = (bf16[128,512,1]{1,0,2:T(8,128)(2,1)S(1)}, bf16[128,512,1]{1,0,2:T(8,128)(2,1)}, u32[]{:S(2)}) copy-start(bf16[128,512,1]{1,0,2:T(8,128)(2,1)} %copy-done.14) | copy-start | bytes 393220
  1266.7 49.4 %copy-start.18 = (bf16[2048,64]{0,1:T(8,128)(2,1)S(1)}, bf16[2048,64]{0,1:T(8,128)(2,1)}, u32[]{:S(2)}) copy-start(bf16[2048,64]{0,1:T(8,128)(2,1)} %param.18) | copy-start | bytes 786436
  1266.7 49.4 %copy-start.22 = (bf16[128,32]{0,1:T(8,128)(2,1)S(1)}, bf16[128,32]{0,1:T(8,128)(2,1)}, u32[]{:S(2)}) copy-start(bf16[128,32]{0,1:T(8,128)(2,1)} %copy-done.21) | copy-start | bytes 24580
  1623.2 6.8 copy-start.11
  1630.0 24.9 %slice-start = ((s8[16777216]{0:T(1024)(128)(4,1)}), s8[4194304]{0:T(1024)(128)(4,1)S(1)}, s32[]{:S(2)}) async-start(s8[16777216]{0:T(1024)(128)(4,1)} %bitcast.182), calls=%async_computation.9 | async-start | bytes 8388608
  1634.4 19.7 %copy-start.20 = (f32[2048,64]{0,1:T(8,128)S(1)}, f32[2048,64]{0,1:T(8,128)}, u32[]{:S(2)}) copy-start(f32[2048,64]{0,1:T(8,128)} %get-tuple-element.753) | copy-start | bytes 1572868
  1634.4 20.5 %slice-start.1 = ((s8[16777216]{0:T(1024)(128)(4,1)}), s8[4194304]{0:T(1024)(128)(4,1)S(1)}, s32[]{:S(2)}) async-start(s8[16777216]{0:T(1024)(128)(4,1)} %bitcast.182), calls=%async_computation.10 | async-start | bytes 8388608
  1634.4 20.5 %slice-start.2 = ((s8[16777216]{0:T(1024)(128)(4,1)}), s8[4194304]{0:T(1024)(128)(4,1)S(1)}, s32[]{:S(2)}) async-start(s8[16777216]{0:T(1024)(128)(4,1)} %bitcast.182), calls=%async_computation.11 | async-start | bytes 8388608
  1634.4 20.5 %slice-start.3 = ((s8[16777216]{0:T(1024)(128)(4,1)}), s8[4194304]{0:T(1024)(128)(4,1)S(1)}, s32[]{:S(2)}) async-start(s8[16777216]{0:T(1024)(128)(4,1)} %bitcast.182), calls=%async_computation.12 | async-start | bytes 8388608
  (13 other events, 42.5 us)
Sparse Core Ops, SparseCore 0:
  13.8 73.6 all-gather.2
  90.2 66.6 all-gather.4
  235.4 685.5 reduce-scatter.7
  924.5 157.0 reduce-scatter.3
  1085.3 156.2 reduce-scatter.5
  1253.7 364.1 all-reduce.2
where the time goes:
time: 1680 us; the launch traced here: 1670 us
  waiting for transfers between devices  1370 us (82%)
  matrix products  110 us (7%)
  blocking collectives  83.4 us (5%)
  local copies, waits for them, and re-layouts  79.9 us (5%)
    reduce_scatter x1, waiting for transfers between devices, device_fn(): lax.psum_scatter(dk_rope_all, 'cp', scatter_dimension=0, tiled=True)  661 us
    psum x1, waiting for transfers between devices, device_fn(): lax.psum((gw_q, gw_dkv, gg_kv, gw_kr, gw_uk, gw_uv, gw_o), 'cp')  301 us
    reduce_scatter x1, waiting for transfers between devices, device_fn(): lax.psum_scatter(dk_nope_all, 'cp', scatter_dimension=0, tiled=True)  159 us
    reduce_scatter x1, waiting for transfers between devices, device_fn(): lax.psum_scatter(dv_all, 'cp', scatter_dimension=0, tiled=True)  156 us
    all_gather x1, waiting for transfers between devices, device_fn(): v_all = lax.all_gather(v_loc, 'cp', axis=0, tiled=True)  69.4 us
    psum x1, blocking collectives, device_fn(): lax.psum((gw_q, gw_dkv, gg_kv, gw_kr, gw_uk, gw_uv, gw_o), 'cp')  47 us
    unnamed x60, local copies, waits for them, and re-layouts  45.6 us
    all_gather x1, blocking collectives, device_fn(): k_rope_all = lax.all_gather(k_rope, 'cp', axis=0, tiled=True)  36.4 us
  transfers between devices with their start and end apart: 6, of which 6 were waited for; matrix products, arithmetic and copies ran while one was open for 3% of the time, Pallas kernels for 0%

commit v1 on v0

v1 whole, which is shorter than its diff:
```python
import functools

import jax
import jax.numpy as jnp
from jax import lax
from jax.experimental import pallas as pl
from jax.experimental.pallas import tpu as pltpu
from jax.sharding import PartitionSpec as P


ROPE_THETA = 10000.0
NORM_EPS = 1e-6
LOG2E = 1.4426950408889634
MASKED = -1e30
F32 = jnp.float32
BF16 = jnp.bfloat16
OVER_ROWS = (((0,), (0,)), ((), ()))
OVER_COLS = (((1,), (1,)), ((), ()))
LANES = 128
SLOT = 2 * LANES
VMEM_LIMIT = 63 * 1024 * 1024
EVENTS = 36


def compiler_params(**more):
    return pltpu.CompilerParams(vmem_limit_bytes=VMEM_LIMIT, **more)


def cost(flops, bytes_accessed=0, transcendentals=0):
    return pl.CostEstimate(flops=int(flops), bytes_accessed=bytes_accessed, transcendentals=transcendentals)


def struct(shape, dtype=F32):
    return jax.ShapeDtypeStruct(shape, dtype)


def whole(*shape):
    return pl.BlockSpec(shape, lambda *i: (0,) * len(shape))


def rows(count, width):
    return pl.BlockSpec((count, width), lambda i, *_: (i, 0))


def zero(*refs):
    for ref in refs:
        ref[...] = jnp.zeros(ref.shape, ref.dtype)


def exact(a, b):
    return jnp.dot(a, b, preferred_element_type=F32)


def over_rows(a, b):
    return lax.dot_general(a, b, OVER_ROWS, preferred_element_type=F32)


def at_block(index, size):
    return pl.ds(pl.multiple_of(index * size, size), size)


def rope_tables(positions, rope_dim):
    half_dim = rope_dim // 2
    inv_freq = ROPE_THETA ** (-(jnp.arange(half_dim, dtype=F32) * 2.0 / rope_dim))
    angles = positions.astype(F32)[:, None] * inv_freq[None, :]
    return jnp.cos(angles), jnp.sin(angles)


def rope_back(g_in, cos_t, sin_t):
    first_half, second_half = jnp.split(g_in, 2, axis=-1)
    return jnp.concatenate([first_half * cos_t + second_half * sin_t, second_half * cos_t - first_half * sin_t], axis=-1)


def attn_kernel(scale, shard, half, nope, rope, core_ref, x_ref, far_ref, near_ref, w_ref, wt_ref, gain_ref, wkv_ref, g_ref,
                odq_ref, keep_ref, give_ref, latent_ref,
                w2_ref, q_ref, k_ref, v_ref, kt_ref, vt_ref, cm_ref, sm_ref, s_ref, m_ref, l_ref, do_ref, d_ref, acc_ref, dk_ref, dv_ref):
    i = pl.program_id(0)
    n = pl.num_programs(0)
    core = core_ref[0]
    bq = q_ref.shape[0]
    bk = x_ref.shape[0]
    vd = v_ref.shape[1]
    rep = bk // LANES

    def keys(j):
        return at_block(j, bk)

    def wide(x):
        return jnp.concatenate([x] * rep, axis=1)

    def fold(x, op):
        return functools.reduce(op, jnp.split(x, rep, axis=1))

    def swapped(t):
        lane = lax.broadcasted_iota(jnp.int32, t.shape, 1)
        return jnp.where(lane % rope < rope // 2, pltpu.roll(t, LANES - rope // 2, 1), pltpu.roll(t, rope // 2, 1))

    def spread(ref, column):
        ref[...] = jnp.broadcast_to(column, ref.shape)

    @pl.when(i == 0)
    def _():
        w2_ref[...] = wt_ref[...].T
        zero(dk_ref, dv_ref)

    step = near_ref.shape[0]

    def project(b, _):
        r = at_block(b, step)
        t = at_block(i * (bk // step) + b, step)
        x = x_ref[r, :]
        c = exact(x, w_ref[...])
        inv = lax.rsqrt(jnp.sum(c * c, axis=1, keepdims=True) * (1.0 / c.shape[1]) + NORM_EPS)
        latent = (c * inv * gain_ref[...]).astype(BF16)
        latent_ref[r, :] = latent
        kv = exact(latent, wkv_ref[...])
        v_ref[t, :] = kv[:, nope:].astype(BF16)
        qk = exact(x, w2_ref[...])
        far = far_ref[pl.ds(i * (bk // step) + b, 1), :]
        lane = lax.broadcasted_iota(jnp.int32, (step, LANES), 1)
        cos_a, sin_a = far[:, :LANES], far[:, LANES:]
        cos_b, sin_b = near_ref[:, :LANES], near_ref[:, LANES:]
        cos_t = cos_a * cos_b - sin_a * sin_b
        sin_t = sin_a * cos_b + cos_a * sin_b
        sin_t = jnp.where(lane % rope < rope // 2, -sin_t, sin_t)
        turned = qk[:, nope:]
        turned = turned * cos_t + swapped(turned) * sin_t
        k = jnp.concatenate([kv[:, :nope], jnp.where(lane < rope, pltpu.roll(turned, rope, 1), 0.0)], axis=1).astype(BF16)
        k_ref[t, :] = k
        kt_ref[:, t] = k.T
        vt_ref[:, t] = kv[:, nope:].astype(BF16).T
        q = jnp.concatenate([qk[:, :nope], jnp.where(lane < rope, turned, 0.0)], axis=1).astype(BF16)
        for a in range(step // shard):
            to = at_block(b * (step // shard) + a, half)
            lo, hi = slice(a * shard, a * shard + half), slice(a * shard + half, (a + 1) * shard)
            for ref, value in ((q_ref, q), (cm_ref, cos_t), (sm_ref, sin_t)):
                ref[to, :] = jnp.where(core == 0, value[lo], value[hi])
        return 0

    lax.fori_loop(0, bk // step, project, 0)

    m_ref[...] = jnp.full(m_ref.shape, MASKED, F32)

    def scores(j):
        return exact(q_ref[...], kt_ref[:, keys(j)])

    def note(j, s):
        s_ref[:, keys(j)] = s
        m_ref[...] = jnp.maximum(m_ref[...], fold(s, jnp.maximum))

    def full_tile(j, _):
        note(j, scores(j))
        return 0

    lax.fori_loop(0, i, full_tile, 0)
    row = lax.broadcasted_iota(jnp.int32, (bq, bk), 0)
    col = lax.broadcasted_iota(jnp.int32, (bq, bk), 1)
    note(i, jnp.where(col <= (row // half) * shard + core * half + row % half, scores(i), MASKED))

    spread(m_ref, jnp.max(m_ref[...], axis=1, keepdims=True))
    zero(l_ref, acc_ref)

    def prob_tile(j, _):
        r = keys(j)
        p = jnp.exp2((s_ref[:, r] - wide(m_ref[...])) * (scale * LOG2E))
        s_ref[:, r] = p
        l_ref[...] += fold(p, jnp.add)
        acc_ref[:, :vd] += exact(p.astype(BF16), v_ref[r, :])
        return 0

    lax.fori_loop(0, i + 1, prob_tile, 0)

    inv = 1.0 / jnp.sum(l_ref[...], axis=1, keepdims=True)
    o = acc_ref[:, :vd] * inv
    odq_ref[:, :vd] = o.astype(BF16)
    do = g_ref[...].astype(F32)
    spread(d_ref, jnp.sum(do * o, axis=1, keepdims=True) * inv)
    do_ref[...] = (do * inv).astype(BF16)
    zero(acc_ref)

    def back_tile(j, _):
        r = keys(j)
        p = s_ref[:, r]
        dp = exact(do_ref[...], vt_ref[:, r])
        ds = (p * (dp - wide(d_ref[...]))).astype(BF16)
        dv_ref[r, :] += over_rows(p.astype(BF16), do_ref[...])
        dk_ref[r, :] += over_rows(ds, q_ref[...])
        acc_ref[...] += exact(ds, k_ref[r, :])
        return 0

    lax.fori_loop(0, i + 1, back_tile, 0)
    dq = acc_ref[...] * scale
    turned = dq[:, nope:]
    turned = turned * cm_ref[...] - swapped(turned) * sm_ref[...]
    odq_ref[:, vd:vd + nope] = dq[:, :nope].astype(BF16)
    odq_ref[:, vd + nope:] = turned.astype(BF16)

    @pl.when(i == n - 1)
    def _():
        def finish(s, _):
            to = at_block(s, half)
            for ref, side in ((keep_ref, core), (give_ref, 1 - core)):
                r = at_block(2 * s + side, half)
                ref[to, :SLOT] = dk_ref[r, :] * scale
                ref[to, SLOT:] = dv_ref[r, :]
            return 0

        lax.fori_loop(0, dk_ref.shape[0] // shard, finish, 0)


def attention(core, x, far, near, w_dkv, wt, gain, wkv, g, scale, shard, nope, rope, n):
    seq, d_model = x.shape
    rank, vd = w_dkv.shape[1], g.shape[1]
    half, nq, bk = shard // 2, seq // 2, seq // n
    bq = nq // n
    vmem = lambda *shape: pltpu.VMEM(shape, F32)
    packed = lambda *shape: pltpu.VMEM(shape, BF16)
    return pl.pallas_call(
        functools.partial(attn_kernel, scale, shard, half, nope, rope),
        grid_spec=pltpu.PrefetchScalarGridSpec(
            num_scalar_prefetch=1, grid=(n,),
            in_specs=[rows(bk, d_model), whole(*far.shape), whole(*near.shape), whole(*w_dkv.shape), whole(*wt.shape), whole(*gain.shape), whole(*wkv.shape), rows(bq, vd)],
            out_specs=[rows(bq, vd + SLOT), whole(nq, SLOT + vd), whole(nq, SLOT + vd), rows(bk, rank)],
            scratch_shapes=[packed(d_model, SLOT), packed(bq, SLOT), packed(seq, SLOT), packed(seq, vd), packed(SLOT, seq), packed(vd, seq),
                            vmem(bq, LANES), vmem(bq, LANES), vmem(bq, seq), vmem(bq, LANES), vmem(bq, LANES), packed(bq, vd), vmem(bq, LANES), vmem(bq, SLOT),
                            vmem(seq, SLOT), vmem(seq, vd)]),
        out_shape=[struct((nq, vd + SLOT), BF16), struct((nq, SLOT + vd)), struct((nq, SLOT + vd)), struct((seq, rank), BF16)],
        compiler_params=compiler_params(),
        cost_estimate=cost(2 * seq * d_model * (rank + SLOT) + 7 * nq * seq * SLOT, 2 * x.size, nq * seq),
    )(core[None], x, far, near, w_dkv, wt, gain, wkv, g)


def ring_kernel(side, counts, make, n_given, n_made, *refs):
    n_ring, n_each, n_same = counts
    total = sum(counts)
    given = refs[:n_given]
    srcs, outs = refs[n_given:n_given + total - n_made], refs[n_given + total - n_made:n_given + 2 * total - n_made]
    send_sem, recv_sem, own_sem, *rest = refs[n_given + 2 * total - n_made:]
    direct_sem, made = rest[:2], rest[2:]
    srcs = [*srcs, *made[:n_made]]
    n_dev = 2 * side * side
    me = lax.axis_index("cp")
    pos = ((me // 2) % side, me // (2 * side))
    mesh_id = pl.DeviceIdType.MESH

    def at(dx, dy):
        return (lax.rem(pos[1] + dy + side, side) * side + lax.rem(pos[0] + dx + side, side)) * 2 + me % 2

    def shifted(color, first, second):
        return at(second, first) if color else at(first, second)

    sibling = me + 1 - 2 * (me % 2)
    direct = n_each + n_same > 0
    neighbours = [shifted(color, d, 0) for color in range(2) for d in (1, -1)]
    peers = [me ^ d for d in range(1, n_dev)] if direct else [*neighbours, sibling]
    barrier = pltpu.get_barrier_semaphore()
    for peer in peers:
        pl.semaphore_signal(barrier, inc=1, device_id={"cp": peer}, device_id_type=mesh_id)
    pl.semaphore_wait(barrier, len(peers))

    def part(ref, color, piece=0, pieces=1):
        size = ref.shape[0] // (2 * pieces)
        return ref.at[pl.ds((pieces * color + piece) * size, size)]

    def copy(src, dst, sems, peer):
        return pltpu.make_async_remote_copy(src_ref=src, dst_ref=dst, send_sem=sems[0], recv_sem=sems[1], device_id={"cp": peer}, device_id_type=mesh_id)

    def sems(k, color, event):
        return send_sem.at[k, color, event], recv_sem.at[k, color, event]

    pending = []

    def send(color, event, block, peer, *piece):
        for k in range(n_ring):
            src, dst = (srcs[k], outs[k].at[me]) if block is None else (outs[k].at[block],) * 2
            pending.append(copy(part(src, color, *piece), part(dst, color, *piece), sems(k, color, event), peer))
            pending[-1].start()

    def arrived(color, event, block, *piece):
        for k in range(n_ring):
            ref = part(outs[k].at[block], color, *piece)
            copy(ref, ref, sems(k, color, event), sibling).wait_recv()

    own = [pltpu.make_async_copy(srcs[k].at[me] if n_ring <= k < n_ring + n_each else srcs[k], outs[k].at[me], own_sem.at[k]) for k in range(total)]
    straight = []
    for k in range(n_ring, total):
        for d in range(1, n_dev):
            peer = me ^ d
            src = srcs[k].at[peer] if k < n_ring + n_each else srcs[k]
            straight.append(copy(src, outs[k].at[me], [s.at[k - n_ring, d] for s in direct_sem], peer))
    late = own[n_ring:] + straight
    if not make:
        late, early = [], own + straight
    else:
        early = own[:n_ring]
    for c in early:
        c.start()
    finish = make(*given, *made) if make else None

    colors = range(2)
    offsets = (0, -1, 1, 2)
    first_out, relays, second_out, to_sibling, column = 0, 2, 4, 20, 24

    def spread(c, j, block):
        for d, way in enumerate((1, -1)):
            send(c, second_out + 4 * j + d, block, shifted(c, 0, way))
        send(c, to_sibling + j, block, sibling)

    def relay(c, j):
        for d, way in enumerate((1, -1)):
            block = shifted(c, offsets[j], -way)
            arrived(c, second_out + 4 * j + d, block)
            send(c, second_out + relays + 4 * j + d, block, shifted(c, 0, way), d, 2)
            send(c, column + 3 * j + d, block, sibling)

    if not n_ring:
        for c in own + straight:
            c.wait()
        return
    for c in colors:
        for d, way in enumerate((1, -1)):
            send(c, first_out + d, None, shifted(c, way, 0))
        spread(c, 0, None)
    if make:
        finish()
    for c in colors:
        for d, way in enumerate((1, -1)):
            block = shifted(c, -way, 0)
            arrived(c, first_out + d, block)
            send(c, relays + d, block, shifted(c, way, 0), d, 2)
            spread(c, 1 + d, block)
    for c in late:
        c.start()
    for c in colors:
        relay(c, 0)
    for c in colors:
        across = shifted(c, 2, 0)
        for d in range(2):
            arrived(c, relays + d, across, d, 2)
        spread(c, 3, across)
    for j in range(1, 4):
        for c in colors:
            relay(c, j)
    for j in range(4):
        for c in colors:
            across = shifted(c, offsets[j], 2)
            for d in range(2):
                arrived(c, second_out + relays + 4 * j + d, across, d, 2)
            send(c, column + 2 + 3 * j, across, sibling)
    other = sibling - me
    for c in colors:
        for j in range(4):
            arrived(c, to_sibling + j, shifted(c, offsets[j], 0) + other)
            for d in range(3):
                arrived(c, column + 3 * j + d, shifted(c, offsets[j], offsets[1 + d]) + other)
    for c in pending:
        c.wait_send()
    for c in own + straight:
        c.wait()


def ring_gather(n_dev, cid, ring, each=(), same=(), make=None, given=(), scratch=()):
    side = round((n_dev // 2) ** 0.5)
    sent = [*ring, *each, *same]
    n_made = 1 if make else 0
    shapes = [struct(a.shape if len(ring) <= k < len(ring) + len(each) else (n_dev,) + a.shape, a.dtype) for k, a in enumerate(sent)]
    shapes += [struct(a.shape, a.dtype) for a in scratch[:n_made]]
    counts = len(ring), len(each) + n_made, len(same)
    n_direct = sum(counts[1:])
    dma = pltpu.SemaphoreType.DMA
    in_vmem, anywhere = pl.BlockSpec(memory_space=pltpu.VMEM), pl.BlockSpec(memory_space=pl.ANY)
    return pl.pallas_call(
        functools.partial(ring_kernel, side, counts, make, len(given), n_made),
        in_specs=[anywhere] * len(given) + [in_vmem] * len(sent), out_specs=[anywhere] * len(shapes), out_shape=shapes,
        scratch_shapes=[dma((max(len(ring), 1), 2, EVENTS))] * 2 + [dma((len(shapes),))] + [dma((max(n_direct, 1), n_dev))] * 2 + list(scratch),
        compiler_params=compiler_params(collective_id=cid, has_side_effects=True),
        cost_estimate=cost(4e10),
    )(*given, *sent)


def make_d_out(gy_ref, w_ref, blocks_ref, gy_vmem, w_vmem, sems):
    reads = [pltpu.make_async_copy(src, dst, sems.at[k]) for k, (src, dst) in enumerate(((gy_ref, gy_vmem), (w_ref, w_vmem)))]
    for c in reads:
        c.start()

    def compute():
        for c in reads:
            c.wait()
        heads, v_dim = w_ref.shape[:2]
        half = blocks_ref.shape[1]

        def two_heads(b, _):
            w = w_vmem[pl.ds(2 * b, 2)].reshape(2 * v_dim, -1)
            g = lax.dot_general(gy_vmem[...], w, OVER_COLS, preferred_element_type=F32).astype(BF16)
            for h in range(2):
                for core in range(2):
                    blocks_ref[4 * b + 2 * h + core] = g[core * half:(core + 1) * half, h * v_dim:(h + 1) * v_dim]
            return 0

        lax.fori_loop(0, heads // 2, two_heads, 0)

    return compute


def query_grads_kernel(qk_dim, core_ref, x_ref, odq_ref, keep_ref, give_ref, q_acc):
    i = pl.program_id(0)
    core = core_ref[0]
    d_model = x_ref.shape[-1]

    @pl.when(i == 0)
    def _():
        zero(q_acc)

    x = x_ref[...].reshape(-1, d_model)
    dq_t = odq_ref[...].T[-SLOT:][:qk_dim]
    for c in range(4):
        cols = slice(c * d_model // 4, (c + 1) * d_model // 4)
        q_acc[:, cols] += exact(dq_t, x[:, cols])

    @pl.when(i == pl.num_programs(0) - 1)
    def _():
        for ref, side in ((keep_ref, core), (give_ref, 1 - core)):
            ref[...] = q_acc[at_block(side, qk_dim // 2), :]


def output_grads_kernel(core_ref, gy_ref, odq_ref, keep_ref, give_ref, o_acc):
    i = pl.program_id(0)
    core = core_ref[0]
    vd, d_model = o_acc.shape

    @pl.when(i == 0)
    def _():
        zero(o_acc)

    gy = gy_ref[...].reshape(-1, d_model)
    o_t = odq_ref[...].T[:vd]
    for c in range(4):
        cols = slice(c * d_model // 4, (c + 1) * d_model // 4)
        o_acc[:, cols] += exact(o_t, gy[:, cols])

    @pl.when(i == pl.num_programs(0) - 1)
    def _():
        for ref, side in ((keep_ref, core), (give_ref, 1 - core)):
            ref[...] = o_acc[at_block(side, vd // 2), :]


def head_grads(kernel, core, act, odq, n_dev, half, width):
    n = 4
    shards = n_dev // n
    d_model = act.shape[1]
    out = width // 2, d_model
    return pl.pallas_call(
        kernel,
        grid_spec=pltpu.PrefetchScalarGridSpec(
            num_scalar_prefetch=1, grid=(n,),
            in_specs=[pl.BlockSpec((shards, 1, half, d_model), lambda i, c: (i, c[0], 0, 0)), rows(shards * half, odq.shape[1])],
            out_specs=[whole(*out)] * 2, scratch_shapes=[pltpu.VMEM((width, d_model), F32)]),
        out_shape=[struct(out)] * 2, compiler_params=compiler_params(), cost_estimate=cost(act.size * width, act.size),
    )(core[None], act.reshape(n_dev, 2, half, d_model), odq)


def up_grads_kernel(core_ref, latent_ref, kv_ref, keep_ref, give_ref):
    core = core_ref[0]
    up = over_rows(latent_ref[...].reshape(-1, latent_ref.shape[-1]), kv_ref[...])
    count = keep_ref.shape[0]
    width = up.shape[1]
    blocks = keep_ref.shape[1] // width
    for a in range(blocks):
        lo, hi = (up[(s * blocks + a) * count:(s * blocks + a + 1) * count] for s in range(2))
        cols = slice(a * width, (a + 1) * width)
        keep_ref[:, cols] = jnp.where(core == 0, lo, hi)
        give_ref[:, cols] = jnp.where(core == 0, hi, lo)


def up_grads(core, latent, kv, d_model, n_dev, half):
    rank, width = latent.shape[1], kv.shape[1]
    out = rank * width // (2 * d_model), d_model
    return pl.pallas_call(
        up_grads_kernel,
        grid_spec=pltpu.PrefetchScalarGridSpec(
            num_scalar_prefetch=1, grid=(1,),
            in_specs=[pl.BlockSpec((n_dev, 1, half, rank), lambda i, c: (0, c[0], 0, 0)), whole(*kv.shape)], out_specs=[whole(*out)] * 2),
        out_shape=[struct(out)] * 2, compiler_params=compiler_params(), cost_estimate=cost(2 * kv.size * rank, latent.size),
    )(core[None], latent.reshape(n_dev, 2, half, rank), kv)


def low_grads_kernel(x_ref, low_ref, dkv_ref, kr_ref, low_t):
    @pl.when(pl.program_id(0) == 0)
    def _():
        count = low_ref.shape[0] // 8

        def turn(b, _):
            r = at_block(b, count)
            low_t[:, r] = low_ref[r, :].T
            return 0

        lax.fori_loop(0, 8, turn, 0)

    g = exact(low_t[...], x_ref[...])
    rank = dkv_ref.shape[1]
    dkv_ref[...] = g[:rank].T
    kr_ref[...] = g[rank:]


def low_grads(x, low, rank, rope):
    seq, d_model = x.shape
    return pl.pallas_call(
        low_grads_kernel, grid=(d_model // SLOT,),
        in_specs=[pl.BlockSpec((seq, SLOT), lambda i: (0, i)), whole(*low.shape)],
        out_specs=[rows(SLOT, rank), pl.BlockSpec((rope, SLOT), lambda i: (0, i))],
        out_shape=[struct((d_model, rank)), struct((rope, d_model))],
        scratch_shapes=[pltpu.VMEM(low.shape[::-1], BF16)],
        compiler_params=compiler_params(), cost_estimate=cost(2 * x.size * (rank + rope), 2 * x.size),
    )(x, low)


def copy_kernel(src_ref, dst_ref):
    dst_ref[...] = src_ref[...]


def copied(a):
    block = rows(a.shape[0] // 8, a.shape[1])
    return pl.pallas_call(copy_kernel, grid=(8,), in_specs=[block], out_specs=block, out_shape=struct(a.shape, a.dtype),
                          compiler_params=compiler_params(), cost_estimate=cost(1e9, 8 * a.size))(a)


def spread_heads_kernel(up_ref, uk_ref, uv_ref):
    heads, _, count, cols = up_ref.shape
    for a, block in enumerate(jnp.split(up_ref[...].reshape(heads, count, cols), cols // SLOT, axis=2)):
        for ref, value in zip((uk_ref, uv_ref), jnp.split(block, 2, axis=2)):
            ref[a * count:(a + 1) * count] = jnp.swapaxes(value, 0, 1)


def spread_heads(up, rank, width):
    heads, _, count, cols = up.shape
    steps = 2
    return pl.pallas_call(
        spread_heads_kernel, grid=(2, steps),
        in_specs=[pl.BlockSpec((heads, 1, count, cols // steps), lambda s, a: (0, s, 0, a))],
        out_specs=[pl.BlockSpec((rank // (2 * steps), heads, width), lambda s, a: (s * steps + a, 0, 0))] * 2,
        out_shape=[struct((rank, heads, width))] * 2, compiler_params=compiler_params(), cost_estimate=cost(1e9, 8 * up.size),
    )(up)


def solution(mesh):
    n_dev = mesh.shape['cp']
    row_spec, per_group = P(('dp', 'cp')), P('dp')
    siblings = [(i, i ^ 1) for i in range(n_dev)]

    def block(x_loc, gy_loc, w_q, w_dkv, g_kv, w_kr, w_uk, w_uv, w_o):
        shard, d_model = x_loc.shape
        heads, qk_dim = w_q.shape[1:]
        rank, _, nope = w_uk.shape
        v_dim, rope = w_uv.shape[2], w_kr.shape[1]
        half, seq = shard // 2, n_dev * shard
        me = lax.axis_index('cp')
        head, core = me // 2, me % 2

        def gather(a):
            return lax.all_gather(a, 'cp', axis=0, tiled=True)

        def summed(keep, give):
            return keep + lax.ppermute(give, 'cp', siblings)

        packed = lambda *shape: pltpu.VMEM(shape, BF16)
        scratch = packed(n_dev, half, v_dim), packed(*gy_loc.shape), packed(*w_o.shape), pltpu.SemaphoreType.DMA((2,))
        x_all, d_out = ring_gather(n_dev, 1, [x_loc], make=make_d_out, given=[gy_loc, w_o], scratch=scratch)
        x_all, d_out = x_all.reshape(seq, d_model), d_out.reshape(seq // 2, v_dim)
        gy_all = gather(lax.optimization_barrier((gy_loc, x_all))[0])

        pick = lambda a, axis: lax.dynamic_index_in_dim(a, head, axis, False)
        wt = jnp.concatenate([pick(w_q.transpose(1, 2, 0), 0), w_kr.T], axis=0)
        wkv = jnp.concatenate([pick(w_uk, 1), pick(w_uv, 1)], axis=1)
        w_uk, w_uv, _ = lax.optimization_barrier((w_uk, w_uv, x_all))

        def table(positions):
            return jnp.concatenate([t for t in rope_tables(positions, rope) for _ in range(4)], axis=1)

        far, near = table(jnp.arange(0, seq, 4 * shard)), table(jnp.arange(4 * shard))
        gain = g_kv.astype(F32)[None]
        odq, kv_keep, kv_give, latent = attention(core, x_all, far, near, w_dkv, wt, gain, wkv, d_out, qk_dim ** -0.5, shard, nope, rope, 4)

        q_keep, q_give = head_grads(functools.partial(query_grads_kernel, qk_dim), core, x_all, odq, n_dev, half, qk_dim)
        gwq = gather(summed(q_keep, q_give))

        kv_sum = lax.optimization_barrier((summed(kv_keep, kv_give), q_keep))[0]
        kv_my = jnp.concatenate([kv_sum[:, :nope], kv_sum[:, SLOT:]], axis=1).astype(BF16)
        dkr_my = kv_sum[:, nope:qk_dim].reshape(n_dev, half * rope // LANES, LANES)
        got = lax.all_to_all(jnp.concatenate([odq, kv_my], axis=1).reshape(n_dev, half, -1), 'cp', 0, 0, tiled=True)
        o_keep, o_give = head_grads(output_grads_kernel, core, gy_all, odq, n_dev, half, v_dim)
        o_my = summed(o_keep, o_give)
        gwo = gather(o_my)
        up_keep, up_give = up_grads(core, latent, kv_my, d_model, n_dev, half)
        up_my = summed(up_keep, up_give)
        got_r, = ring_gather(n_dev, 2, [], [lax.optimization_barrier((dkr_my, o_my, up_my))[0]])

        got, got_r = lax.optimization_barrier((got, got_r))
        dkr_loc = jnp.sum(got_r.reshape(heads, shard, rope), axis=0)
        got = got.reshape(heads, shard, -1)
        o_loc, dq_loc, _, dk_loc, dv_loc = jnp.split(got, [v_dim, v_dim + qk_dim, v_dim + SLOT, v_dim + SLOT + nope], axis=2)
        y_loc = jnp.einsum('htv,hvd->td', o_loc, w_o, preferred_element_type=F32).astype(BF16)
        d_latent = jnp.einsum('htn,chn->tc', dk_loc, w_uk, preferred_element_type=F32) + jnp.einsum('htv,chv->tc', dv_loc, w_uv, preferred_element_type=F32)
        c_loc = exact(x_loc, w_dkv)
        inv_loc = lax.rsqrt(jnp.mean(c_loc * c_loc, axis=-1, keepdims=True) + NORM_EPS)
        c_norm = c_loc * inv_loc
        gg_part = jnp.sum(d_latent * c_norm, axis=0)
        d_norm = d_latent * gain
        dc_loc = (inv_loc * (d_norm - c_norm * jnp.mean(d_norm * c_norm, axis=-1, keepdims=True))).astype(BF16)
        cos_t, sin_t = rope_tables(me * shard + jnp.arange(shard), rope)
        dkr_raw = rope_back(dkr_loc, cos_t, sin_t).astype(BF16)
        dx_loc = jnp.einsum('hte,dhe->td', dq_loc, w_q, preferred_element_type=F32) + jnp.einsum('tc,dc->td', dc_loc, w_dkv, preferred_element_type=F32) + jnp.einsum('tr,dr->td', dkr_raw, w_kr, preferred_element_type=F32)

        gg_rows = rank // LANES
        gg_part = jnp.pad(gg_part.reshape(gg_rows, LANES), ((0, 8 - gg_rows), (0, 0)))
        low, up, gg = ring_gather(n_dev, 3, [jnp.concatenate([dc_loc, dkr_raw], axis=1), up_my], (), [gg_part])
        gw_dkv, gw_kr = low_grads(x_all, low.reshape(seq, rank + rope), rank, rope)
        gg_kv = jnp.sum(gg, axis=0)[:gg_rows].reshape(rank)
        gwq = copied(gwq)
        gw_uk, gw_uv = spread_heads(up.reshape(heads, 2, -1, d_model), rank, nope)
        gw_q = gwq.reshape(heads, qk_dim, d_model).transpose(2, 0, 1)
        return y_loc, dx_loc.astype(BF16), gw_q, gw_dkv, gg_kv, gw_kr.T, gw_uk, gw_uv, gwo.reshape(heads, v_dim, d_model)

    return jax.shard_map(block, mesh=mesh, in_specs=(row_spec, row_spec) + (P(),) * 7, out_specs=(row_spec, row_spec) + (per_group,) * 7, check_vma=False)
```

time: 1680 us -> 409 us (0.24)
  waiting for transfers between devices: 1370 us -> 8.21 us
  Pallas kernels: 0 us -> 318 us
  matrix products: 110 us -> 21.7 us
  blocking collectives: 83.4 us -> 0 us
  local copies, waits for them, and re-layouts: 79.9 us -> 23.3 us
    reduce_scatter x3 -> x0, waiting for transfers between devices: 976 us -> none  [the longest x1 661 us: device_fn(): lax.psum_scatter(dk_rope_all, 'cp', scatter_dimension=0, tiled=True)]
    pallas_call x0 -> x10, Pallas kernels: none -> 318 us  [the longest x3 206 us: ring_gather(): pl.pallas_call(functools.partial(ring_kernel, side, counts, make, len(giv...]
    psum x1 -> x0, waiting for transfers between devices: 301 us -> none  [device_fn(): lax.psum((gw_q, gw_dkv, gg_kv, gw_kr, gw_uk, gw_uv, gw_o), 'cp')]
    all_gather x2 -> x3, waiting for transfers between devices: 93.8 us -> 0.02 us  [gather(): return lax.all_gather(a, 'cp', axis=0, tiled=True)]
    dot_general x39 -> x7, matrix products: 104 us -> 21.7 us  [the longest x1 7.08 us: block(): jnp.einsum('hte,dhe->td', dq_loc, w_q, preferred_element_type=F32)]
    psum x1 -> x0, blocking collectives: 47 us -> none  [device_fn(): lax.psum((gw_q, gw_dkv, gg_kv, gw_kr, gw_uk, gw_uv, gw_o), 'cp')]
    all_gather x1 -> x0, blocking collectives: 36.4 us -> none  [device_fn(): k_rope_all = lax.all_gather(k_rope, 'cp', axis=0, tiled=True)]
    unnamed x60 -> x23, local copies, waits for them, and re-layouts: 45.6 us -> 14.3 us
  transfers between devices with their start and end apart: 6 -> 8, of which waited for: 6 -> 3; matrix products, arithmetic and copies ran while one was open for 3% -> 12% of each run, Pallas kernels for 0% -> 62%
where the time goes in v1:
time: 409 us; the launch traced here: 407 us
  Pallas kernels  318 us (78%)
  local copies, waits for them, and re-layouts  23.3 us (6%)
  matrix products  21.7 us (5%)
  other arithmetic  17.3 us (4%)
  between operations  14.1 us (3%)
  waiting for transfers between devices  8.21 us (2%)
  starting transfers between devices  5.02 us (1%)
    pallas_call x3, Pallas kernels, ring_gather(): pl.pallas_call(functools.partial(ring_kernel, side, counts, make, len(giv...  206 us
    pallas_call x1, Pallas kernels, attention(): pl.pallas_call(functools.partial(attn_kernel, scale, shard, half, nope, r...  50.8 us
    pallas_call x1, Pallas kernels, low_grads(): pl.pallas_call(low_grads_kernel, grid=(d_model // SLOT,), in_specs=[pl.Bl...  18.6 us
    pallas_call x1, Pallas kernels, copied(): pl.pallas_call(copy_kernel, grid=(8,), in_specs=[block], out_specs=block,...  18.3 us
    unnamed x23, local copies, waits for them, and re-layouts  14.3 us
    pallas_call x2, Pallas kernels, head_grads(): pl.pallas_call(kernel, grid_spec=pltpu.PrefetchScalarGridSpec(num_scalar_...  13.1 us
  transfers between devices with their start and end apart: 8, of which 3 were waited for; matrix products, arithmetic and copies ran while one was open for 12% of the time, Pallas kernels for 62%

profile of v1, /device:TPU:97, one launch (start us, length us, event | category | flops | bytes accessed | tf_op | source)
XLA Modules:
  0.0 407.5 jit_solution(10544719185569243821)
XLA Ops:
  7.3 63.4 %shard_map.160 = (bf16[32,128,2048]{2,1,0:T(8,128)(2,1)}, bf16[32,64,128]{2,1,0:T(8,128)(2,1)}) custom-call(bf16[128,2048]{1,0:T(8,128)(2,1)} %refs_0_.1, bf16[16,128,2048]{2,1,0:T(8,128)(2,1)} %refs_1_.1, bf16[128,2048]{1,0:T(8,128)(2,1)} %refs_2_.1), custom_call_target="tpu_custom_call" | custom-call | flops 40000000000 | tf_op jit(solution)/shard_map/pallas_call | solution.py:372
  71.7 2.1 constant_dynamic-slice_fusion
  80.2 50.8 %shard_map.161 = (bf16[2048,384]{1,0:T(8,128)(2,1)}, f32[2048,384]{1,0:T(8,128)}, f32[2048,384]{1,0:T(8,128)}, bf16[4096,512]{1,0:T(8,128)(2,1)}) custom-call(s32[1]{0:T(128)} %bitcast.core_ref, bf16[4096,2048]{1,0:T(8,128)(2,1)} %bitcast.50, f32[8,256]{1,0:T(8,128)} %concatenate.28.far_ref, f32[512,256]{1,0:T(8,128)} %concatenate.29.near_ref, ...), custom_call_target="tpu_custom_call" | custom-call | flops 27917287424 | bytes 16777216 | tf_op jit(solution)/shard_map/pallas_call | solution.py:218
  131.0 6.9 %shard_map.162 = (f32[96,2048]{1,0:T(8,128)}, f32[96,2048]{1,0:T(8,128)}) custom-call(s32[1]{0:T(128)} %bitcast.core_ref, bf16[32,2,64,2048]{3,2,1,0:T(8,128)(2,1)} %bitcast.51, bf16[2048,384]{1,0:T(8,128)(2,1)} %get-tuple-element.37.odq_ref), custom_call_target="tpu_custom_call" | custom-call | flops 1610612736 | bytes 8388608 | tf_op jit(solution)/shard_map/pallas_call | solution.py:452
  137.9 2.5 collective-permute-done.3
  140.4 2.1 add.72
  142.6 6.2 %shard_map.163 = (f32[64,2048]{1,0:T(8,128)}, f32[64,2048]{1,0:T(8,128)}) custom-call(s32[1]{0:T(128)} %bitcast.core_ref, bf16[32,2,64,2048]{3,2,1,0:T(8,128)(2,1)} %bitcast.54, bf16[2048,384]{1,0:T(8,128)(2,1)} %get-tuple-element.37.odq_ref), custom_call_target="tpu_custom_call" | custom-call | flops 1073741824 | bytes 8388608 | tf_op jit(solution)/shard_map/pallas_call | solution.py:452
  149.0 2.0 collective-permute-done.1
  153.2 2.3 multiply_reduce_fusion.2
  155.6 3.5 collective-permute-done
  159.1 2.2 add.61
  164.9 3.4 shard_map.164
  168.5 3.3 pad_maximum_fusion
  171.8 4.1 %all-to-all-start = ((bf16[32,64,640]{2,1,0:T(8,128)(2,1)}), bf16[32,64,640]{2,1,0:T(8,128)(2,1)}, u32[]{:S(2)}, u32[]{:S(2)}) async-start(bf16[32,64,640]{2,1,0:T(8,128)(2,1)} %bitcast.55), calls=%async_computation | async-start | bytes 5242880 | tf_op jit(solution)/shard_map/all_to_all | solution.py:589
  177.7 74.4 %shard_map.165 = f32[32,32,128]{2,1,0:T(8,128)} custom-call(f32[32,32,128]{2,1,0:T(8,128)} %reshape.96.refs_0_), custom_call_target="tpu_custom_call" | custom-call | flops 40000000000 | tf_op jit(solution)/shard_map/pallas_call | solution.py:372
  253.5 2.7 fusion.6
  256.3 2.0 multiply_reduce_fusion
  260.1 68.1 %shard_map.167 = (bf16[32,128,576]{2,1,0:T(8,128)(2,1)}, f32[32,32,2048]{2,1,0:T(8,128)}, f32[32,8,128]{2,1,0:T(8,128)}) custom-call(bf16[128,576]{1,0:T(8,128)(2,1)} %pad_maximum_fusion.4.refs_0_, f32[32,2048]{1,0:T(8,128)} %add.63.refs_1_, f32[8,128]{1,0:T(8,128)} %pad.4.refs_2_), custom_call_target="tpu_custom_call" | custom-call | flops 40000000000 | tf_op jit(solution)/shard_map/pallas_call | solution.py:372
  329.2 7.6 %shard_map.169 = (f32[512,16,128]{2,1,0:T(8,128)}, f32[512,16,128]{2,1,0:T(8,128)}) custom-call(f32[16,2,32,2048]{3,2,1,0:T(8,128)} %bitcast.56), custom_call_target="tpu_custom_call" | custom-call | flops 1000000000 | bytes 16777216 | tf_op jit(solution)/shard_map/pallas_call | solution.py:537
  337.4 7.1 %convolution_bitcast_fusion.1 = f32[128,2048]{1,0:T(8,128)S(1)} fusion(bf16[2048,16,192]{0,2,1:T(8,128)(2,1)} %param.11, bf16[16,128,640]{2,1,0:T(8,128)(2,1)} %bitcast.13), kind=kOutput, calls=%fused_computation.4 | convolution fusion | flops 1610612736 | bytes 14680064 | tf_op jit(solution)/shard_map/hte,dhe->td/dot_general | solution.py:611
  346.6 5.6 %fusion = bf16[128,2048]{1,0:T(8,128)(2,1)} fusion(bf16[16,128,2048]{2,1,0:T(8,128)(2,1)} %refs_1_.1, bf16[16,128,640]{2,1,0:T(8,128)(2,1)} %bitcast.13), kind=kOutput, calls=%fused_computation.5 | convolution fusion | flops 1074003968 | bytes 9437184 | tf_op jit(solution)/shard_map/htv,hvd->td/dot_general | solution.py:601
  352.3 18.6 %shard_map.168 = (f32[2048,512]{1,0:T(8,128)}, f32[64,2048]{1,0:T(8,128)}) custom-call(bf16[4096,2048]{1,0:T(8,128)(2,1)} %bitcast.52, bf16[4096,576]{1,0:T(8,128)(2,1)} %bitcast.63), custom_call_target="tpu_custom_call" | custom-call | flops 9663676416 | bytes 16777216 | tf_op jit(solution)/shard_map/pallas_call | solution.py:507
  370.8 18.3 %shard_map.166 = f32[3072,2048]{1,0:T(8,128)} custom-call(f32[3072,2048]{1,0:T(8,128)} %all-gather.6.cloned.1.call-done.src_ref), custom_call_target="tpu_custom_call" | custom-call | flops 1000000000 | bytes 50331648 | tf_op jit(solution)/shard_map/pallas_call | solution.py:523
  389.1 11.8 %copy.53 = f32[16,128,2048]{2,1,0:T(8,128)} copy(f32[16,128,2048]{2,1,0:T(8,128)} %bitcast.53) | data formatting | bytes 33554432
  (69 shorter events, 22.1 us)
Async XLA Ops:
  7.2 63.9 %copy-start.9 = (bf16[512]{0:T(512)(128)(2,1)S(1)}, bf16[512]{0:T(512)(128)(2,1)}, u32[]{:S(2)}) copy-start(bf16[512]{0:T(512)(128)(2,1)} %param.13) | copy-start | bytes 3076
  7.2 135.4 %all-gather.4.cloned.1.call-start = ((), (), s32[]{:S(2)}) async-start(), calls=%async_computation.1 | async-start | bytes 17301504 | tf_op jit(solution)/shard_map/all_gather | solution.py:560
  70.8 300.0 %all-gather.6.cloned.1.call-start = ((), (), s32[]{:S(2)}) async-start(), calls=%async_computation.2 | async-start | bytes 25952256 | tf_op jit(solution)/shard_map/all_gather | solution.py:560
  74.6 4.5 %copy-start.4 = (bf16[2048,64]{0,1:T(8,128)(2,1)S(1)}, bf16[2048,64]{0,1:T(8,128)(2,1)}, u32[]{:S(2)}) copy-start(bf16[2048,64]{0,1:T(8,128)(2,1)} %param.14) | copy-start | bytes 786436
  137.9 2.5 collective-permute-start.3
  142.5 246.6 %all-gather.8.cloned.1.call-start = ((), (), s32[]{:S(2)}) async-start(), calls=%async_computation.3 | async-start | bytes 17301504 | tf_op jit(solution)/shard_map/all_gather | solution.py:560
  148.8 10.2 %copy-start.3 = (f32[2048,384]{1,0:T(8,128)S(1)}, f32[2048,384]{1,0:T(8,128)}, u32[]{:S(2)}) copy-start(f32[2048,384]{1,0:T(8,128)} %get-tuple-element.38) | copy-start | bytes 9437188
  148.9 2.1 collective-permute-start.1
  153.0 6.1 %collective-permute-start = (f32[2048,384]{1,0:T(8,128)}, f32[2048,384]{1,0:T(8,128)}, u32[]{:S(2)}, u32[]{:S(2)}) collective-permute-start(f32[2048,384]{1,0:T(8,128)} %get-tuple-element.39), channel_id=1, source_target_pairs={{0,1},{1,0},{2,3},{3,2},{4,5},{5,4},{6,7},{7,6},{8,9},{9,8},{10,11... | collective-permute-start | bytes 9437192 | tf_op jit(solution)/shard_map/ppermute | solution.py:563
  161.3 1.7 copy-start
  163.1 0.8 copy-start.2
  168.4 8.6 %collective-permute-start.2 = (f32[32,2048]{1,0:T(8,128)}, f32[32,2048]{1,0:T(8,128)S(1)}, u32[]{:S(2)}, u32[]{:S(2)}) collective-permute-start(f32[32,2048]{1,0:T(8,128)} %get-tuple-element.47), channel_id=1, source_target_pairs={{0,1},{1,0},{2,3},{3,2},{4,5},{5,4},{6,7},{7,6},{8,9},{9,8},{10,11... | collective-permute-start | bytes 786440 | tf_op jit(solution)/shard_map/ppermute | solution.py:563
  171.8 4.1 %slice-start = ((f32[2048,384]{1,0:T(8,128)}), f32[2048,64]{1,0:T(8,128)S(1)}, s32[]{:S(2)}) async-start(f32[2048,384]{1,0:T(8,128)} %copy-done), calls=%async_computation.4 | async-start | bytes 2097152 | tf_op jit(solution)/shard_map/slice | solution.py:588
  171.8 5.1 %copy-start.6 = (f32[32,2048]{1,0:T(8,128)S(1)}, f32[32,2048]{1,0:T(8,128)}, u32[]{:S(2)}) copy-start(f32[32,2048]{1,0:T(8,128)} %get-tuple-element.46) | copy-start | bytes 786436
  171.8 80.3 %all-to-all-start = ((bf16[32,64,640]{2,1,0:T(8,128)(2,1)}), bf16[32,64,640]{2,1,0:T(8,128)(2,1)}, u32[]{:S(2)}, u32[]{:S(2)}) async-start(bf16[32,64,640]{2,1,0:T(8,128)(2,1)} %bitcast.55), calls=%async_computation | async-start | bytes 5242880 | tf_op jit(solution)/shard_map/all_to_all | solution.py:589
  253.4 2.9 copy-start.8
  253.5 2.8 copy-start.7
  337.4 7.1 %copy-start.1 = (bf16[2048,512]{1,0:T(8,128)(2,1)S(1)}, bf16[2048,512]{1,0:T(8,128)(2,1)}, u32[]{:S(2)}) copy-start(bf16[2048,512]{1,0:T(8,128)(2,1)} %w_ref.1) | copy-start | bytes 6291460
  344.5 1.0 copy-start.5
Sparse Core Ops, SparseCore 0:
  70.9 66.3 all-gather.3
  142.6 119.4 all-gather.5
  264.2 82.6 all-gather.7

commit v2 on v1

--- a/solution.py
+++ b/solution.py
@@ -2,6 +2,7 @@
 
 import jax
 import jax.numpy as jnp
+import numpy as np
 from jax import lax
 from jax.experimental import pallas as pl
 from jax.experimental.pallas import tpu as pltpu
@@ -55,15 +56,19 @@
     return lax.dot_general(a, b, OVER_ROWS, preferred_element_type=F32)
 
 
+def over_cols(a, b):
+    return lax.dot_general(a, b, OVER_COLS, preferred_element_type=F32)
+
+
 def at_block(index, size):
     return pl.ds(pl.multiple_of(index * size, size), size)
 
 
-def rope_tables(positions, rope_dim):
+def rope_tables(positions, rope_dim, xp=jnp):
     half_dim = rope_dim // 2
-    inv_freq = ROPE_THETA ** (-(jnp.arange(half_dim, dtype=F32) * 2.0 / rope_dim))
-    angles = positions.astype(F32)[:, None] * inv_freq[None, :]
-    return jnp.cos(angles), jnp.sin(angles)
+    inv_freq = ROPE_THETA ** (-(xp.arange(half_dim, dtype=xp.float32) * 2.0 / rope_dim))
+    angles = positions[:, None] * inv_freq[None, :]
+    return xp.cos(angles), xp.sin(angles)
 
 
 def rope_back(g_in, cos_t, sin_t):
@@ -71,12 +76,12 @@
     return jnp.concatenate([first_half * cos_t + second_half * sin_t, second_half * cos_t - first_half * sin_t], axis=-1)
 
 
-def attn_kernel(scale, shard, half, nope, rope, core_ref, x_ref, far_ref, near_ref, w_ref, wt_ref, gain_ref, wkv_ref, g_ref,
+def attn_kernel(scale, shard, half, nope, rope, place_ref, x_ref, far_ref, near_ref, w_ref, wq_ref, wr_ref, gain_ref, uk_ref, uv_ref, g_ref,
                 odq_ref, keep_ref, give_ref, latent_ref,
-                w2_ref, q_ref, k_ref, v_ref, kt_ref, vt_ref, cm_ref, sm_ref, s_ref, m_ref, l_ref, do_ref, d_ref, acc_ref, dk_ref, dv_ref):
+                w2_ref, wkv_ref, q_ref, k_ref, v_ref, cm_ref, sm_ref, s_ref, m_ref, l_ref, do_ref, d_ref, acc_ref, dk_ref, dv_ref):
     i = pl.program_id(0)
     n = pl.num_programs(0)
-    core = core_ref[0]
+    core = place_ref[0]
     bq = q_ref.shape[0]
     bk = x_ref.shape[0]
     vd = v_ref.shape[1]
@@ -95,12 +100,19 @@
         lane = lax.broadcasted_iota(jnp.int32, t.shape, 1)
         return jnp.where(lane % rope < rope // 2, pltpu.roll(t, LANES - rope // 2, 1), pltpu.roll(t, rope // 2, 1))
 
+    def both_tables(t):
+        first = lax.broadcasted_iota(jnp.int32, t.shape, 1) < rope
+        other = pltpu.roll(t, rope, 1)
+        return jnp.where(first, t, other), jnp.where(first, other, t)
+
     def spread(ref, column):
         ref[...] = jnp.broadcast_to(column, ref.shape)
 
     @pl.when(i == 0)
     def _():
-        w2_ref[...] = wt_ref[...].T
+        w2_ref[...] = jnp.concatenate([wq_ref[0], wr_ref[...]], axis=0).T
+        wkv_ref[:, :nope] = uk_ref[...]
+        wkv_ref[:, nope:] = uv_ref[...]
         zero(dk_ref, dv_ref)
 
     step = near_ref.shape[0]
@@ -118,17 +130,13 @@
         qk = exact(x, w2_ref[...])
         far = far_ref[pl.ds(i * (bk // step) + b, 1), :]
         lane = lax.broadcasted_iota(jnp.int32, (step, LANES), 1)
-        cos_a, sin_a = far[:, :LANES], far[:, LANES:]
-        cos_b, sin_b = near_ref[:, :LANES], near_ref[:, LANES:]
+        (cos_a, sin_a), (cos_b, sin_b) = both_tables(far), both_tables(near_ref[...])
         cos_t = cos_a * cos_b - sin_a * sin_b
         sin_t = sin_a * cos_b + cos_a * sin_b
         sin_t = jnp.where(lane % rope < rope // 2, -sin_t, sin_t)
         turned = qk[:, nope:]
         turned = turned * cos_t + swapped(turned) * sin_t
-        k = jnp.concatenate([kv[:, :nope], jnp.where(lane < rope, pltpu.roll(turned, rope, 1), 0.0)], axis=1).astype(BF16)
-        k_ref[t, :] = k
-        kt_ref[:, t] = k.T
-        vt_ref[:, t] = kv[:, nope:].astype(BF16).T
+        k_ref[t, :] = jnp.concatenate([kv[:, :nope], jnp.where(lane < rope, pltpu.roll(turned, rope, 1), 0.0)], axis=1).astype(BF16)
         q = jnp.concatenate([qk[:, :nope], jnp.where(lane < rope, turned, 0.0)], axis=1).astype(BF16)
         for a in range(step // shard):
             to = at_block(b * (step // shard) + a, half)
@@ -142,7 +150,7 @@
     m_ref[...] = jnp.full(m_ref.shape, MASKED, F32)
 
     def scores(j):
-        return exact(q_ref[...], kt_ref[:, keys(j)])
+        return over_cols(q_ref[...], k_ref[keys(j), :])
 
     def note(j, s):
         s_ref[:, keys(j)] = s
@@ -181,7 +189,7 @@
     def back_tile(j, _):
         r = keys(j)
         p = s_ref[:, r]
-        dp = exact(do_ref[...], vt_ref[:, r])
+        dp = over_cols(do_ref[...], v_ref[r, :])
         ds = (p * (dp - wide(d_ref[...]))).astype(BF16)
         dv_ref[r, :] += over_rows(p.astype(BF16), do_ref[...])
         dk_ref[r, :] += over_rows(ds, q_ref[...])
@@ -208,7 +216,7 @@
         lax.fori_loop(0, dk_ref.shape[0] // shard, finish, 0)
 
 
-def attention(core, x, far, near, w_dkv, wt, gain, wkv, g, scale, shard, nope, rope, n):
+def attention(place, x, far, near, w_dkv, wq, wr, gain, uk, uv, g, scale, shard, nope, rope, n):
     seq, d_model = x.shape
     rank, vd = w_dkv.shape[1], g.shape[1]
     half, nq, bk = shard // 2, seq // 2, seq // n
@@ -219,15 +227,16 @@
         functools.partial(attn_kernel, scale, shard, half, nope, rope),
         grid_spec=pltpu.PrefetchScalarGridSpec(
             num_scalar_prefetch=1, grid=(n,),
-            in_specs=[rows(bk, d_model), whole(*far.shape), whole(*near.shape), whole(*w_dkv.shape), whole(*wt.shape), whole(*gain.shape), whole(*wkv.shape), rows(bq, vd)],
+            in_specs=[rows(bk, d_model), whole(*far.shape), whole(*near.shape), whole(*w_dkv.shape), pl.BlockSpec((1, *wq.shape[1:]), lambda i, c: (c[1], 0, 0)),
+                      whole(*wr.shape), whole(*gain.shape), whole(*uk.shape), whole(*uv.shape), rows(bq, vd)],
             out_specs=[rows(bq, vd + SLOT), whole(nq, SLOT + vd), whole(nq, SLOT + vd), rows(bk, rank)],
-            scratch_shapes=[packed(d_model, SLOT), packed(bq, SLOT), packed(seq, SLOT), packed(seq, vd), packed(SLOT, seq), packed(vd, seq),
+            scratch_shapes=[packed(d_model, SLOT), packed(rank, nope + vd), packed(bq, SLOT), packed(seq, SLOT), packed(seq, vd),
                             vmem(bq, LANES), vmem(bq, LANES), vmem(bq, seq), vmem(bq, LANES), vmem(bq, LANES), packed(bq, vd), vmem(bq, LANES), vmem(bq, SLOT),
                             vmem(seq, SLOT), vmem(seq, vd)]),
         out_shape=[struct((nq, vd + SLOT), BF16), struct((nq, SLOT + vd)), struct((nq, SLOT + vd)), struct((seq, rank), BF16)],
         compiler_params=compiler_params(),
         cost_estimate=cost(2 * seq * d_model * (rank + SLOT) + 7 * nq * seq * SLOT, 2 * x.size, nq * seq),
-    )(core[None], x, far, near, w_dkv, wt, gain, wkv, g)
+    )(place, x, far, near, w_dkv, wq, wr, gain, uk, uv, g)
 
 
 def ring_kernel(side, counts, make, n_given, n_made, *refs):
@@ -252,11 +261,25 @@
     sibling = me + 1 - 2 * (me % 2)
     direct = n_each + n_same > 0
     neighbours = [shifted(color, d, 0) for color in range(2) for d in (1, -1)]
-    peers = [me ^ d for d in range(1, n_dev)] if direct else [*neighbours, sibling]
     barrier = pltpu.get_barrier_semaphore()
-    for peer in peers:
+
+    def greet(peer):
         pl.semaphore_signal(barrier, inc=1, device_id={"cp": peer}, device_id_type=mesh_id)
-    pl.semaphore_wait(barrier, len(peers))
+
+    def others(do):
+        def body(d, _):
+            do(d)
+            return 0
+
+        lax.fori_loop(1, n_dev, body, 0)
+
+    if direct:
+        others(lambda d: greet(me ^ d))
+        pl.semaphore_wait(barrier, n_dev - 1)
+    else:
+        for peer in (*neighbours, sibling):
+            greet(peer)
+        pl.semaphore_wait(barrier, len(neighbours) + 1)
 
     def part(ref, color, piece=0, pieces=1):
         size = ref.shape[0] // (2 * pieces)
@@ -282,19 +305,28 @@
             copy(ref, ref, sems(k, color, event), sibling).wait_recv()
 
     own = [pltpu.make_async_copy(srcs[k].at[me] if n_ring <= k < n_ring + n_each else srcs[k], outs[k].at[me], own_sem.at[k]) for k in range(total)]
-    straight = []
-    for k in range(n_ring, total):
-        for d in range(1, n_dev):
-            peer = me ^ d
-            src = srcs[k].at[peer] if k < n_ring + n_each else srcs[k]
-            straight.append(copy(src, outs[k].at[me], [s.at[k - n_ring, d] for s in direct_sem], peer))
-    late = own[n_ring:] + straight
+
+    def straight(d):
+        for k in range(n_ring, total):
+            src = srcs[k].at[me ^ d] if k < n_ring + n_each else srcs[k]
+            yield copy(src, outs[k].at[me], [s.at[k - n_ring, d] for s in direct_sem], me ^ d)
+
+    def start_direct():
+        for c in own[n_ring:]:
+            c.start()
+        if direct:
+            others(lambda d: [c.start() for c in straight(d)])
+
+    def wait_all():
+        for c in own:
+            c.wait()
+        if direct:
+            others(lambda d: [c.wait() for c in straight(d)])
+
+    for c in own[:n_ring]:
+        c.start()
     if not make:
-        late, early = [], own + straight
-    else:
-        early = own[:n_ring]
-    for c in early:
-        c.start()
+        start_direct()
     finish = make(*given, *made) if make else None
 
     colors = range(2)
@@ -314,30 +346,29 @@
             send(c, column + 3 * j + d, block, sibling)
 
     if not n_ring:
-        for c in own + straight:
-            c.wait()
+        wait_all()
         return
     for c in colors:
         for d, way in enumerate((1, -1)):
             send(c, first_out + d, None, shifted(c, way, 0))
         spread(c, 0, None)
-    if make:
-        finish()
     for c in colors:
         for d, way in enumerate((1, -1)):
             block = shifted(c, -way, 0)
             arrived(c, first_out + d, block)
             send(c, relays + d, block, shifted(c, way, 0), d, 2)
             spread(c, 1 + d, block)
-    for c in late:
-        c.start()
     for c in colors:
         relay(c, 0)
+    if make:
+        finish()
     for c in colors:
         across = shifted(c, 2, 0)
         for d in range(2):
             arrived(c, relays + d, across, d, 2)
         spread(c, 3, across)
+    if make:
+        start_direct()
     for j in range(1, 4):
         for c in colors:
             relay(c, j)
@@ -355,8 +386,7 @@
                 arrived(c, column + 3 * j + d, shifted(c, offsets[j], offsets[1 + d]) + other)
     for c in pending:
         c.wait_send()
-    for c in own + straight:
-        c.wait()
+    wait_all()
 
 
 def ring_gather(n_dev, cid, ring, each=(), same=(), make=None, given=(), scratch=()):
@@ -391,7 +421,7 @@
 
         def two_heads(b, _):
             w = w_vmem[pl.ds(2 * b, 2)].reshape(2 * v_dim, -1)
-            g = lax.dot_general(gy_vmem[...], w, OVER_COLS, preferred_element_type=F32).astype(BF16)
+            g = over_cols(gy_vmem[...], w).astype(BF16)
             for h in range(2):
                 for core in range(2):
                     blocks_ref[4 * b + 2 * h + core] = g[core * half:(core + 1) * half, h * v_dim:(h + 1) * v_dim]
@@ -487,14 +517,9 @@
 def low_grads_kernel(x_ref, low_ref, dkv_ref, kr_ref, low_t):
     @pl.when(pl.program_id(0) == 0)
     def _():
-        count = low_ref.shape[0] // 8
-
-        def turn(b, _):
-            r = at_block(b, count)
-            low_t[:, r] = low_ref[r, :].T
-            return 0
-
-        lax.fori_loop(0, 8, turn, 0)
+        n_dev, _, shard = low_ref.shape
+        for d in range(n_dev):
+            low_t[:, d * shard:(d + 1) * shard] = low_ref[d]
 
     g = exact(low_t[...], x_ref[...])
     rank = dkv_ref.shape[1]
@@ -502,15 +527,18 @@
     kr_ref[...] = g[rank:]
 
 
-def low_grads(x, low, rank, rope):
+def low_grads(x, low, rank):
     seq, d_model = x.shape
+    width = low.shape[1]
+    rope = width - rank
+    cols = 2 * SLOT
     return pl.pallas_call(
-        low_grads_kernel, grid=(d_model // SLOT,),
-        in_specs=[pl.BlockSpec((seq, SLOT), lambda i: (0, i)), whole(*low.shape)],
-        out_specs=[rows(SLOT, rank), pl.BlockSpec((rope, SLOT), lambda i: (0, i))],
+        low_grads_kernel, grid=(d_model // cols,),
+        in_specs=[pl.BlockSpec((seq, cols), lambda i: (0, i)), whole(*low.shape)],
+        out_specs=[rows(cols, rank), pl.BlockSpec((rope, cols), lambda i: (0, i))],
         out_shape=[struct((d_model, rank)), struct((rope, d_model))],
-        scratch_shapes=[pltpu.VMEM(low.shape[::-1], BF16)],
-        compiler_params=compiler_params(), cost_estimate=cost(2 * x.size * (rank + rope), 2 * x.size),
+        scratch_shapes=[pltpu.VMEM((width, seq), BF16)],
+        compiler_params=compiler_params(), cost_estimate=cost(2 * x.size * width, 2 * x.size),
     )(x, low)
 
 
@@ -519,8 +547,9 @@
 
 
 def copied(a):
-    block = rows(a.shape[0] // 8, a.shape[1])
-    return pl.pallas_call(copy_kernel, grid=(8,), in_specs=[block], out_specs=block, out_shape=struct(a.shape, a.dtype),
+    steps = 4
+    block = rows(a.shape[0] // steps, a.shape[1])
+    return pl.pallas_call(copy_kernel, grid=(steps,), in_specs=[block], out_specs=block, out_shape=struct(a.shape, a.dtype),
                           compiler_params=compiler_params(), cost_estimate=cost(1e9, 8 * a.size))(a)
 
 
@@ -569,36 +598,42 @@
         gy_all = gather(lax.optimization_barrier((gy_loc, x_all))[0])
 
         pick = lambda a, axis: lax.dynamic_index_in_dim(a, head, axis, False)
-        wt = jnp.concatenate([pick(w_q.transpose(1, 2, 0), 0), w_kr.T], axis=0)
-        wkv = jnp.concatenate([pick(w_uk, 1), pick(w_uv, 1)], axis=1)
+        uk, uv = pick(w_uk, 1), pick(w_uv, 1)
         w_uk, w_uv, _ = lax.optimization_barrier((w_uk, w_uv, x_all))
 
         def table(positions):
-            return jnp.concatenate([t for t in rope_tables(positions, rope) for _ in range(4)], axis=1)
-
-        far, near = table(jnp.arange(0, seq, 4 * shard)), table(jnp.arange(4 * shard))
+            return np.concatenate([t for t in rope_tables(positions.astype(np.float32), rope, np) for _ in range(LANES // rope)], axis=1)
+
+        far, near = table(np.arange(0, seq, 4 * shard)), table(np.arange(4 * shard))
         gain = g_kv.astype(F32)[None]
-        odq, kv_keep, kv_give, latent = attention(core, x_all, far, near, w_dkv, wt, gain, wkv, d_out, qk_dim ** -0.5, shard, nope, rope, 4)
-
+        odq, kv_keep, kv_give, latent = attention(jnp.stack([core, head]), x_all, far, near, w_dkv, w_q.transpose(1, 2, 0), w_kr.T, gain, uk, uv, d_out, qk_dim ** -0.5, shard, nope, rope, 4)
+
+        def exchange(a):
+            return lax.all_to_all(a.reshape(n_dev, half, -1), 'cp', 0, 0, tiled=True).reshape(heads, shard, -1)
+
+        got_odq = exchange(odq)
         q_keep, q_give = head_grads(functools.partial(query_grads_kernel, qk_dim), core, x_all, odq, n_dev, half, qk_dim)
-        gwq = gather(summed(q_keep, q_give))
+        q_my = summed(q_keep, q_give)
+        gwq = gather(q_my)
 
         kv_sum = lax.optimization_barrier((summed(kv_keep, kv_give), q_keep))[0]
         kv_my = jnp.concatenate([kv_sum[:, :nope], kv_sum[:, SLOT:]], axis=1).astype(BF16)
         dkr_my = kv_sum[:, nope:qk_dim].reshape(n_dev, half * rope // LANES, LANES)
-        got = lax.all_to_all(jnp.concatenate([odq, kv_my], axis=1).reshape(n_dev, half, -1), 'cp', 0, 0, tiled=True)
         o_keep, o_give = head_grads(output_grads_kernel, core, gy_all, odq, n_dev, half, v_dim)
         o_my = summed(o_keep, o_give)
         gwo = gather(o_my)
+        got_odq, kv_my, _ = lax.optimization_barrier((got_odq, kv_my, o_keep))
+        got_kv = exchange(kv_my)
         up_keep, up_give = up_grads(core, latent, kv_my, d_model, n_dev, half)
         up_my = summed(up_keep, up_give)
-        got_r, = ring_gather(n_dev, 2, [], [lax.optimization_barrier((dkr_my, o_my, up_my))[0]])
-
-        got, got_r = lax.optimization_barrier((got, got_r))
+        o_loc, dq_loc, _ = jnp.split(got_odq, [v_dim, v_dim + qk_dim], axis=2)
+        y_loc = jnp.einsum('htv,hvd->td', o_loc, w_o, preferred_element_type=F32).astype(BF16)
+        dx_loc = jnp.einsum('hte,dhe->td', dq_loc, w_q, preferred_element_type=F32)
+        dkr_my, y_loc, dx_loc, _, _ = lax.optimization_barrier((dkr_my, y_loc, dx_loc, o_my, up_my))
+        got_r, = ring_gather(n_dev, 2, [], [dkr_my])
+        got_kv, got_r = lax.optimization_barrier((got_kv, got_r))
         dkr_loc = jnp.sum(got_r.reshape(heads, shard, rope), axis=0)
-        got = got.reshape(heads, shard, -1)
-        o_loc, dq_loc, _, dk_loc, dv_loc = jnp.split(got, [v_dim, v_dim + qk_dim, v_dim + SLOT, v_dim + SLOT + nope], axis=2)
-        y_loc = jnp.einsum('htv,hvd->td', o_loc, w_o, preferred_element_type=F32).astype(BF16)
+        dk_loc, dv_loc = jnp.split(got_kv, [nope], axis=2)
         d_latent = jnp.einsum('htn,chn->tc', dk_loc, w_uk, preferred_element_type=F32) + jnp.einsum('htv,chv->tc', dv_loc, w_uv, preferred_element_type=F32)
         c_loc = exact(x_loc, w_dkv)
         inv_loc = lax.rsqrt(jnp.mean(c_loc * c_loc, axis=-1, keepdims=True) + NORM_EPS)
@@ -606,14 +641,14 @@
         gg_part = jnp.sum(d_latent * c_norm, axis=0)
         d_norm = d_latent * gain
         dc_loc = (inv_loc * (d_norm - c_norm * jnp.mean(d_norm * c_norm, axis=-1, keepdims=True))).astype(BF16)
-        cos_t, sin_t = rope_tables(me * shard + jnp.arange(shard), rope)
+        cos_t, sin_t = rope_tables((me * shard + jnp.arange(shard)).astype(F32), rope)
         dkr_raw = rope_back(dkr_loc, cos_t, sin_t).astype(BF16)
-        dx_loc = jnp.einsum('hte,dhe->td', dq_loc, w_q, preferred_element_type=F32) + jnp.einsum('tc,dc->td', dc_loc, w_dkv, preferred_element_type=F32) + jnp.einsum('tr,dr->td', dkr_raw, w_kr, preferred_element_type=F32)
+        dx_loc = dx_loc + jnp.einsum('tc,dc->td', dc_loc, w_dkv, preferred_element_type=F32) + jnp.einsum('tr,dr->td', dkr_raw, w_kr, preferred_element_type=F32)
 
         gg_rows = rank // LANES
         gg_part = jnp.pad(gg_part.reshape(gg_rows, LANES), ((0, 8 - gg_rows), (0, 0)))
-        low, up, gg = ring_gather(n_dev, 3, [jnp.concatenate([dc_loc, dkr_raw], axis=1), up_my], (), [gg_part])
-        gw_dkv, gw_kr = low_grads(x_all, low.reshape(seq, rank + rope), rank, rope)
+        low, up, gg = ring_gather(n_dev, 3, [jnp.concatenate([dc_loc, dkr_raw], axis=1).T, up_my], (), [gg_part])
+        gw_dkv, gw_kr = low_grads(x_all, low, rank)
         gg_kv = jnp.sum(gg, axis=0)[:gg_rows].reshape(rank)
         gwq = copied(gwq)
         gw_uk, gw_uv = spread_heads(up.reshape(heads, 2, -1, d_model), rank, nope)

time: 409 us -> 379 us (0.927)
  Pallas kernels: 318 us -> 273 us
  waiting for transfers between devices: 8.21 us -> 27.8 us
  local copies, waits for them, and re-layouts: 23.3 us -> 19.2 us
    pallas_call x3, Pallas kernels: 206 us -> 164 us  [ring_gather(): pl.pallas_call(functools.partial(ring_kernel, side, counts, make, len(giv...]
    all_to_all x1 -> x2, waiting for transfers between devices: 0.01 us -> 22 us  [exchange(): lax.all_to_all(a.reshape(n_dev, half, -1), 'cp', 0, 0, tiled=True)]
    concatenate x4 -> x0, other arithmetic: 5.89 us -> none  [the longest x1 3.34 us: block(): jnp.concatenate([odq, kv_my], axis=1).reshape(n_dev, half, -1)]
    unnamed x23 -> x25, local copies, waits for them, and re-layouts: 14.3 us -> 13.3 us
  transfers between devices with their start and end apart: 8 -> 9, of which waited for: 3 -> 4; matrix products, arithmetic and copies ran while one was open for 12% -> 11% of each run, Pallas kernels for 62% -> 56%
where the time goes in v2:
time: 379 us; the launch traced here: 378 us
  Pallas kernels  273 us (72%)
  waiting for transfers between devices  27.8 us (7%)
  matrix products  21.2 us (6%)
  local copies, waits for them, and re-layouts  19.2 us (5%)
  between operations  14.1 us (4%)
  other arithmetic  13.5 us (4%)
  starting transfers between devices  8.98 us (2%)
    pallas_call x3, Pallas kernels, ring_gather(): pl.pallas_call(functools.partial(ring_kernel, side, counts, make, len(giv...  164 us
    pallas_call x1, Pallas kernels, attention(): pl.pallas_call(functools.partial(attn_kernel, scale, shard, half, nope, r...  51 us
    all_to_all x2, waiting for transfers between devices, exchange(): lax.all_to_all(a.reshape(n_dev, half, -1), 'cp', 0, 0, tiled=True)  22 us
    pallas_call x1, Pallas kernels, low_grads(): pl.pallas_call(low_grads_kernel, grid=(d_model // cols,), in_specs=[pl.Bl...  17.4 us
    pallas_call x1, Pallas kernels, copied(): pl.pallas_call(copy_kernel, grid=(steps,), in_specs=[block], out_specs=bl...  16.5 us
    unnamed x25, local copies, waits for them, and re-layouts  13.3 us
    pallas_call x2, Pallas kernels, head_grads(): pl.pallas_call(kernel, grid_spec=pltpu.PrefetchScalarGridSpec(num_scalar_...  13.3 us
    dot_general x1, matrix products, block(): dx_loc = jnp.einsum('hte,dhe->td', dq_loc, w_q, preferred_element_type=F32)  10.1 us
  transfers between devices with their start and end apart: 9, of which 4 were waited for; matrix products, arithmetic and copies ran while one was open for 11% of the time, Pallas kernels for 56%

profile of v2, /device:TPU:97, one launch (start us, length us, event | category | flops | bytes accessed | tf_op | source)
XLA Modules:
  0.0 378.1 jit_solution(15466009499981604127)
XLA Ops:
  7.3 63.6 %shard_map.178 = (bf16[32,128,2048]{2,1,0:T(8,128)(2,1)}, bf16[32,64,128]{2,1,0:T(8,128)(2,1)}) custom-call(bf16[128,2048]{1,0:T(8,128)(2,1)} %refs_0_.1, bf16[16,128,2048]{2,1,0:T(8,128)(2,1)} %refs_1_.1, bf16[128,2048]{1,0:T(8,128)(2,1)} %refs_2_.1), custom_call_target="tpu_custom_call" | custom-call | flops 40000000000 | tf_op jit(solution)/shard_map/pallas_call | solution.py:402
  71.6 2.1 constant_dynamic-slice_fusion
  75.6 51.0 %shard_map.179 = (bf16[2048,384]{1,0:T(8,128)(2,1)}, f32[2048,384]{1,0:T(8,128)}, f32[2048,384]{1,0:T(8,128)}, bf16[4096,512]{1,0:T(8,128)(2,1)}) custom-call(s32[2]{0:T(128)} %pad_add_fusion.place_ref, bf16[4096,2048]{1,0:T(8,128)(2,1)} %bitcast.53, f32[8,128]{1,0:T(8,128)} %constant.58.clone.far_ref, f32[512,128]{1,0:T(8,128)} %constant.59.clone.near_ref, ...), custom_call_target="tpu_custom_call" | custom-call | flops 27917287424 | bytes 16777216 | tf_op jit(solution)/shard_map/pallas_call | solution.py:226
  126.6 7.0 %shard_map.180 = (f32[96,2048]{1,0:T(8,128)}, f32[96,2048]{1,0:T(8,128)}) custom-call(s32[1]{0:T(128)} %bitcast.core_ref, bf16[32,2,64,2048]{3,2,1,0:T(8,128)(2,1)} %bitcast.54, bf16[2048,384]{1,0:T(8,128)(2,1)} %get-tuple-element.43.odq_ref), custom_call_target="tpu_custom_call" | custom-call | flops 1610612736 | bytes 8388608 | tf_op jit(solution)/shard_map/pallas_call | solution.py:482
  133.7 2.5 collective-permute-done.3
  136.1 2.1 add.70
  138.4 6.2 %shard_map.181 = (f32[64,2048]{1,0:T(8,128)}, f32[64,2048]{1,0:T(8,128)}) custom-call(s32[1]{0:T(128)} %bitcast.core_ref, bf16[32,2,64,2048]{3,2,1,0:T(8,128)(2,1)} %bitcast.57, bf16[2048,384]{1,0:T(8,128)(2,1)} %get-tuple-element.43.odq_ref), custom_call_target="tpu_custom_call" | custom-call | flops 1073741824 | bytes 8388608 | tf_op jit(solution)/shard_map/pallas_call | solution.py:482
  144.8 2.0 collective-permute-done.1
  146.7 2.0 add.60
  149.1 3.9 %all-to-all-start = ((bf16[32,64,384]{2,1,0:T(8,128)(2,1)}), bf16[32,64,384]{2,1,0:T(8,128)(2,1)}, u32[]{:S(2)}, u32[]{:S(2)}) async-start(bf16[32,64,384]{2,1,0:T(8,128)(2,1)} %bitcast.10), calls=%async_computation | async-start | bytes 3145728 | tf_op jit(solution)/shard_map/all_to_all | solution.py:612
  154.9 3.3 add.59
  160.6 22.0 %all-to-all-done = bf16[32,64,384]{2,1,0:T(8,128)(2,1)} async-done(((bf16[32,64,384]{2,1,0:T(8,128)(2,1)}), bf16[32,64,384]{2,1,0:T(8,128)(2,1)}, u32[]{:S(2)}, u32[]{:S(2)}) %all-to-all-start) | async-done | bytes 1572896 | tf_op jit(solution)/shard_map/all_to_all | solution.py:612
  182.6 3.4 shard_map.182
  186.8 10.1 %convolution_bitcast_fusion.1 = f32[128,2048]{1,0:T(8,128)} fusion(bf16[2048,16,192]{0,2,1:T(8,128)(2,1)} %param.13, bf16[16,128,384]{2,1,0:T(8,128)(2,1)} %bitcast.11), kind=kOutput, calls=%fused_computation.1 | convolution fusion | flops 1610612736 | bytes 14680064 | tf_op jit(solution)/shard_map/hte,dhe->td/dot_general | solution.py:631
  196.9 3.1 fusion
  200.0 3.7 all-to-all-start.1
  204.4 40.5 %shard_map.183 = f32[32,32,128]{2,1,0:T(8,128)} custom-call(f32[32,32,128]{2,1,0:T(8,128)} %reshape.89.refs_0_), custom_call_target="tpu_custom_call" | custom-call | flops 40000000000 | tf_op jit(solution)/shard_map/pallas_call | solution.py:402
  246.5 2.6 fusion.5
  252.6 60.1 %shard_map.185 = (bf16[32,576,128]{2,1,0:T(8,128)(2,1)}, f32[32,32,2048]{2,1,0:T(8,128)}, f32[32,8,128]{2,1,0:T(8,128)}) custom-call(bf16[576,128]{1,0:T(8,128)(2,1)} %maximum_bitcast_fusion.refs_0_, f32[32,2048]{1,0:T(8,128)} %add.61.refs_1_, f32[8,128]{1,0:T(8,128)} %pad.4.refs_2_), custom_call_target="tpu_custom_call" | custom-call | flops 40000000000 | tf_op jit(solution)/shard_map/pallas_call | solution.py:402
  313.7 7.7 %shard_map.187 = (f32[512,16,128]{2,1,0:T(8,128)}, f32[512,16,128]{2,1,0:T(8,128)}) custom-call(f32[16,2,32,2048]{3,2,1,0:T(8,128)} %bitcast.58), custom_call_target="tpu_custom_call" | custom-call | flops 1000000000 | bytes 16777216 | tf_op jit(solution)/shard_map/pallas_call | solution.py:566
  322.2 2.6 fusion.33
  325.8 17.4 %shard_map.186 = (f32[2048,512]{1,0:T(8,128)}, f32[64,2048]{1,0:T(8,128)}) custom-call(bf16[4096,2048]{1,0:T(8,128)(2,1)} %bitcast.55, bf16[32,576,128]{2,1,0:T(8,128)(2,1)} %get-tuple-element.62.low_ref), custom_call_target="tpu_custom_call" | custom-call | flops 9663676416 | bytes 16777216 | tf_op jit(solution)/shard_map/pallas_call | solution.py:535
  343.2 16.5 %shard_map.184 = f32[3072,2048]{1,0:T(8,128)} custom-call(f32[3072,2048]{1,0:T(8,128)} %all-gather.6.cloned.1.call-done.src_ref), custom_call_target="tpu_custom_call" | custom-call | flops 1000000000 | bytes 50331648 | tf_op jit(solution)/shard_map/pallas_call | solution.py:552
  359.8 11.8 %copy.70 = f32[16,128,2048]{2,1,0:T(8,128)} copy(f32[16,128,2048]{2,1,0:T(8,128)} %bitcast.56) | data formatting | bytes 33554432
  (67 shorter events, 16.9 us)
Async XLA Ops:
  7.2 63.8 %copy-start.7 = (bf16[512]{0:T(512)(128)(2,1)S(1)}, bf16[512]{0:T(512)(128)(2,1)}, u32[]{:S(2)}) copy-start(bf16[512]{0:T(512)(128)(2,1)} %param.15) | copy-start | bytes 3076
  7.2 131.2 %all-gather.4.cloned.1.call-start = ((), (), s32[]{:S(2)}) async-start(), calls=%async_computation.2 | async-start | bytes 17301504 | tf_op jit(solution)/shard_map/all_gather | solution.py:589
  70.9 272.3 %all-gather.6.cloned.1.call-start = ((), (), s32[]{:S(2)}) async-start(), calls=%async_computation.3 | async-start | bytes 25952256 | tf_op jit(solution)/shard_map/all_gather | solution.py:589
  133.6 2.5 collective-permute-start.3
  138.3 221.5 %all-gather.8.cloned.1.call-start = ((), (), s32[]{:S(2)}) async-start(), calls=%async_computation.4 | async-start | bytes 17301504 | tf_op jit(solution)/shard_map/all_gather | solution.py:589
  144.6 2.1 collective-permute-start.1
  148.7 4.2 %copy-start = (bf16[2048,512]{1,0:T(8,128)(2,1)S(1)}, bf16[2048,512]{1,0:T(8,128)(2,1)}, u32[]{:S(2)}) copy-start(bf16[2048,512]{1,0:T(8,128)(2,1)} %w_ref.1) | copy-start | bytes 6291460
  148.7 4.3 %copy-start.2 = (bf16[128,2048]{1,0:T(8,128)(2,1)S(1)}, bf16[128,2048]{1,0:T(8,128)(2,1)}, u32[]{:S(2)}) copy-start(bf16[128,2048]{1,0:T(8,128)(2,1)} %refs_2_.1) | copy-start | bytes 1572868
  148.8 6.1 %collective-permute-start = (f32[2048,384]{1,0:T(8,128)}, f32[2048,384]{1,0:T(8,128)}, u32[]{:S(2)}, u32[]{:S(2)}) collective-permute-start(f32[2048,384]{1,0:T(8,128)} %get-tuple-element.42), channel_id=1, source_target_pairs={{0,1},{1,0},{2,3},{3,2},{4,5},{5,4},{6,7},{7,6},{8,9},{9,8},{10,11... | collective-permute-start | bytes 9437192 | tf_op jit(solution)/shard_map/ppermute | solution.py:592
  149.1 33.5 %all-to-all-start = ((bf16[32,64,384]{2,1,0:T(8,128)(2,1)}), bf16[32,64,384]{2,1,0:T(8,128)(2,1)}, u32[]{:S(2)}, u32[]{:S(2)}) async-start(bf16[32,64,384]{2,1,0:T(8,128)(2,1)} %bitcast.10), calls=%async_computation | async-start | bytes 3145728 | tf_op jit(solution)/shard_map/all_to_all | solution.py:612
  186.0 10.9 %slice-start = ((s8[8388608]{0:T(1024)(128)(4,1)}), s8[4194304]{0:T(1024)(128)(4,1)S(1)}, s32[]{:S(2)}) async-start(s8[8388608]{0:T(1024)(128)(4,1)} %bitcast.51), calls=%async_computation.5 | async-start | bytes 8388608
  186.0 10.9 %slice-start.1 = ((s8[8388608]{0:T(1024)(128)(4,1)}), s8[4194304]{0:T(1024)(128)(4,1)S(1)}, s32[]{:S(2)}) async-start(s8[8388608]{0:T(1024)(128)(4,1)} %bitcast.51), calls=%async_computation.6 | async-start | bytes 8388608
  186.0 17.7 %collective-permute-start.2 = (f32[32,2048]{1,0:T(8,128)}, f32[32,2048]{1,0:T(8,128)S(1)}, u32[]{:S(2)}, u32[]{:S(2)}) collective-permute-start(f32[32,2048]{1,0:T(8,128)} %get-tuple-element.53), channel_id=1, source_target_pairs={{0,1},{1,0},{2,3},{3,2},{4,5},{5,4},{6,7},{7,6},{8,9},{9,8},{10,11... | collective-permute-start | bytes 786440 | tf_op jit(solution)/shard_map/ppermute | solution.py:592
  200.0 3.7 copy-start.3
  200.0 45.0 %all-to-all-start.1 = ((bf16[32,64,256]{2,1,0:T(8,128)(2,1)}), bf16[32,64,256]{2,1,0:T(8,128)(2,1)}, u32[]{:S(2)}, u32[]{:S(2)}) async-start(bf16[32,64,256]{2,1,0:T(8,128)(2,1)} %bitcast.16), calls=%async_computation.1 | async-start | bytes 2097152 | tf_op jit(solution)/shard_map/all_to_all | solution.py:612
  246.3 2.8 copy-start.6
  246.4 2.8 copy-start.5
  313.7 8.2 %copy-start.4 = (bf16[2048,64]{0,1:T(8,128)(2,1)S(1)}, bf16[2048,64]{0,1:T(8,128)(2,1)}, u32[]{:S(2)}) copy-start(bf16[2048,64]{0,1:T(8,128)(2,1)} %param.16) | copy-start | bytes 786436
  321.9 3.0 copy-start.1
Sparse Core Ops, SparseCore 0:
  71.0 66.3 all-gather.3
  140.1 119.8 all-gather.5
  262.1 76.4 all-gather.7

commit v3 on v2

--- a/solution.py
+++ b/solution.py
@@ -77,7 +77,7 @@
 
 
 def attn_kernel(scale, shard, half, nope, rope, place_ref, x_ref, far_ref, near_ref, w_ref, wq_ref, wr_ref, gain_ref, uk_ref, uv_ref, g_ref,
-                odq_ref, keep_ref, give_ref, latent_ref,
+                odq_ref, sent_ref, keep_ref, give_ref, latent_ref,
                 w2_ref, wkv_ref, q_ref, k_ref, v_ref, cm_ref, sm_ref, s_ref, m_ref, l_ref, do_ref, d_ref, acc_ref, dk_ref, dv_ref):
     i = pl.program_id(0)
     n = pl.num_programs(0)
@@ -202,6 +202,12 @@
     turned = turned * cm_ref[...] - swapped(turned) * sm_ref[...]
     odq_ref[:, vd:vd + nope] = dq[:, :nope].astype(BF16)
     odq_ref[:, vd + nope:] = turned.astype(BF16)
+    sent_ref[:, :half] = o.astype(BF16).reshape(-1, half, LANES)
+    sent_ref[:, half:2 * half] = dq[:, :nope].astype(BF16).reshape(-1, half, LANES)
+    turned = turned.reshape(-1, half, LANES)
+    low, high = turned[:, :half // 2], turned[:, half // 2:]
+    lane = lax.broadcasted_iota(jnp.int32, low.shape, 2)
+    sent_ref[:, 2 * half:] = jnp.where(lane < rope, low, pltpu.roll(high, rope, 2)).astype(BF16)
 
     @pl.when(i == n - 1)
     def _():
@@ -221,6 +227,7 @@
     rank, vd = w_dkv.shape[1], g.shape[1]
     half, nq, bk = shard // 2, seq // 2, seq // n
     bq = nq // n
+    sent = seq // shard, 2 * half + half // 2, LANES
     vmem = lambda *shape: pltpu.VMEM(shape, F32)
     packed = lambda *shape: pltpu.VMEM(shape, BF16)
     return pl.pallas_call(
@@ -229,11 +236,11 @@
             num_scalar_prefetch=1, grid=(n,),
             in_specs=[rows(bk, d_model), whole(*far.shape), whole(*near.shape), whole(*w_dkv.shape), pl.BlockSpec((1, *wq.shape[1:]), lambda i, c: (c[1], 0, 0)),
                       whole(*wr.shape), whole(*gain.shape), whole(*uk.shape), whole(*uv.shape), rows(bq, vd)],
-            out_specs=[rows(bq, vd + SLOT), whole(nq, SLOT + vd), whole(nq, SLOT + vd), rows(bk, rank)],
+            out_specs=[rows(bq, vd + SLOT), pl.BlockSpec((sent[0] // n, *sent[1:]), lambda i, c: (i, 0, 0)), whole(nq, SLOT + vd), whole(nq, SLOT + vd), rows(bk, rank)],
             scratch_shapes=[packed(d_model, SLOT), packed(rank, nope + vd), packed(bq, SLOT), packed(seq, SLOT), packed(seq, vd),
                             vmem(bq, LANES), vmem(bq, LANES), vmem(bq, seq), vmem(bq, LANES), vmem(bq, LANES), packed(bq, vd), vmem(bq, LANES), vmem(bq, SLOT),
                             vmem(seq, SLOT), vmem(seq, vd)]),
-        out_shape=[struct((nq, vd + SLOT), BF16), struct((nq, SLOT + vd)), struct((nq, SLOT + vd)), struct((seq, rank), BF16)],
+        out_shape=[struct((nq, vd + SLOT), BF16), struct(sent, BF16), struct((nq, SLOT + vd)), struct((nq, SLOT + vd)), struct((seq, rank), BF16)],
         compiler_params=compiler_params(),
         cost_estimate=cost(2 * seq * d_model * (rank + SLOT) + 7 * nq * seq * SLOT, 2 * x.size, nq * seq),
     )(place, x, far, near, w_dkv, wq, wr, gain, uk, uv, g)
@@ -514,7 +521,7 @@
     )(core[None], latent.reshape(n_dev, 2, half, rank), kv)
 
 
-def low_grads_kernel(x_ref, low_ref, dkv_ref, kr_ref, low_t):
+def finish_kernel(x_ref, low_ref, g_ref, dkv_ref, kr_ref, copy_ref, low_t):
     @pl.when(pl.program_id(0) == 0)
     def _():
         n_dev, _, shard = low_ref.shape
@@ -525,32 +532,24 @@
     rank = dkv_ref.shape[1]
     dkv_ref[...] = g[:rank].T
     kr_ref[...] = g[rank:]
-
-
-def low_grads(x, low, rank):
+    copy_ref[...] = g_ref[...]
+
+
+def finish(x, low, g, rank):
     seq, d_model = x.shape
     width = low.shape[1]
     rope = width - rank
-    cols = 2 * SLOT
+    steps = 4
+    cols = d_model // steps
+    piece = rows(g.shape[0] // steps, g.shape[1])
     return pl.pallas_call(
-        low_grads_kernel, grid=(d_model // cols,),
-        in_specs=[pl.BlockSpec((seq, cols), lambda i: (0, i)), whole(*low.shape)],
-        out_specs=[rows(cols, rank), pl.BlockSpec((rope, cols), lambda i: (0, i))],
-        out_shape=[struct((d_model, rank)), struct((rope, d_model))],
+        finish_kernel, grid=(steps,),
+        in_specs=[pl.BlockSpec((seq, cols), lambda i: (0, i)), whole(*low.shape), piece],
+        out_specs=[rows(cols, rank), pl.BlockSpec((rope, cols), lambda i: (0, i)), piece],
+        out_shape=[struct((d_model, rank)), struct((rope, d_model)), struct(g.shape)],
         scratch_shapes=[pltpu.VMEM((width, seq), BF16)],
-        compiler_params=compiler_params(), cost_estimate=cost(2 * x.size * width, 2 * x.size),
-    )(x, low)
-
-
-def copy_kernel(src_ref, dst_ref):
-    dst_ref[...] = src_ref[...]
-
-
-def copied(a):
-    steps = 4
-    block = rows(a.shape[0] // steps, a.shape[1])
-    return pl.pallas_call(copy_kernel, grid=(steps,), in_specs=[block], out_specs=block, out_shape=struct(a.shape, a.dtype),
-                          compiler_params=compiler_params(), cost_estimate=cost(1e9, 8 * a.size))(a)
+        compiler_params=compiler_params(), cost_estimate=cost(2 * x.size * width, 2 * x.size + 8 * g.size),
+    )(x, low, g)
 
 
 def spread_heads_kernel(up_ref, uk_ref, uv_ref):
@@ -606,12 +605,12 @@
 
         far, near = table(np.arange(0, seq, 4 * shard)), table(np.arange(4 * shard))
         gain = g_kv.astype(F32)[None]
-        odq, kv_keep, kv_give, latent = attention(jnp.stack([core, head]), x_all, far, near, w_dkv, w_q.transpose(1, 2, 0), w_kr.T, gain, uk, uv, d_out, qk_dim ** -0.5, shard, nope, rope, 4)
+        odq, sent, kv_keep, kv_give, latent = attention(jnp.stack([core, head]), x_all, far, near, w_dkv, w_q.transpose(1, 2, 0), w_kr.T, gain, uk, uv, d_out, qk_dim ** -0.5, shard, nope, rope, 4)
 
         def exchange(a):
-            return lax.all_to_all(a.reshape(n_dev, half, -1), 'cp', 0, 0, tiled=True).reshape(heads, shard, -1)
-
-        got_odq = exchange(odq)
+            return lax.all_to_all(a, 'cp', 0, 0, tiled=True).reshape(heads, 2, *a.shape[1:])
+
+        got_odq = exchange(sent)
         q_keep, q_give = head_grads(functools.partial(query_grads_kernel, qk_dim), core, x_all, odq, n_dev, half, qk_dim)
         q_my = summed(q_keep, q_give)
         gwq = gather(q_my)
@@ -623,17 +622,19 @@
         o_my = summed(o_keep, o_give)
         gwo = gather(o_my)
         got_odq, kv_my, _ = lax.optimization_barrier((got_odq, kv_my, o_keep))
-        got_kv = exchange(kv_my)
+        got_kv = exchange(kv_my.reshape(n_dev, half, -1))
         up_keep, up_give = up_grads(core, latent, kv_my, d_model, n_dev, half)
         up_my = summed(up_keep, up_give)
-        o_loc, dq_loc, _ = jnp.split(got_odq, [v_dim, v_dim + qk_dim], axis=2)
+        o_loc, dq_loc, dq_rope = jnp.split(got_odq, [half, 2 * half], axis=2)
+        dq_loc = jnp.concatenate([dq_loc, jnp.concatenate([dq_rope[..., :rope], dq_rope[..., rope:]], axis=2)], axis=3)
+        o_loc, dq_loc = o_loc.reshape(heads, shard, -1), dq_loc.reshape(heads, shard, -1)
         y_loc = jnp.einsum('htv,hvd->td', o_loc, w_o, preferred_element_type=F32).astype(BF16)
         dx_loc = jnp.einsum('hte,dhe->td', dq_loc, w_q, preferred_element_type=F32)
         dkr_my, y_loc, dx_loc, _, _ = lax.optimization_barrier((dkr_my, y_loc, dx_loc, o_my, up_my))
         got_r, = ring_gather(n_dev, 2, [], [dkr_my])
         got_kv, got_r = lax.optimization_barrier((got_kv, got_r))
         dkr_loc = jnp.sum(got_r.reshape(heads, shard, rope), axis=0)
-        dk_loc, dv_loc = jnp.split(got_kv, [nope], axis=2)
+        dk_loc, dv_loc = jnp.split(got_kv.reshape(heads, shard, -1), [nope], axis=2)
         d_latent = jnp.einsum('htn,chn->tc', dk_loc, w_uk, preferred_element_type=F32) + jnp.einsum('htv,chv->tc', dv_loc, w_uv, preferred_element_type=F32)
         c_loc = exact(x_loc, w_dkv)
         inv_loc = lax.rsqrt(jnp.mean(c_loc * c_loc, axis=-1, keepdims=True) + NORM_EPS)
@@ -647,12 +648,13 @@
 
         gg_rows = rank // LANES
         gg_part = jnp.pad(gg_part.reshape(gg_rows, LANES), ((0, 8 - gg_rows), (0, 0)))
-        low, up, gg = ring_gather(n_dev, 3, [jnp.concatenate([dc_loc, dkr_raw], axis=1).T, up_my], (), [gg_part])
-        gw_dkv, gw_kr = low_grads(x_all, low, rank)
+        low_my = jnp.concatenate([dc_loc, dkr_raw], axis=1).T
+        low_my, dx_loc = lax.optimization_barrier((low_my, dx_loc.astype(BF16)))
+        low, up, gg = ring_gather(n_dev, 3, [low_my, up_my], (), [gg_part])
+        gw_dkv, gw_kr, gwq = finish(x_all, low, gwq, rank)
         gg_kv = jnp.sum(gg, axis=0)[:gg_rows].reshape(rank)
-        gwq = copied(gwq)
         gw_uk, gw_uv = spread_heads(up.reshape(heads, 2, -1, d_model), rank, nope)
         gw_q = gwq.reshape(heads, qk_dim, d_model).transpose(2, 0, 1)
-        return y_loc, dx_loc.astype(BF16), gw_q, gw_dkv, gg_kv, gw_kr.T, gw_uk, gw_uv, gwo.reshape(heads, v_dim, d_model)
+        return y_loc, dx_loc, gw_q, gw_dkv, gg_kv, gw_kr.T, gw_uk, gw_uv, gwo.reshape(heads, v_dim, d_model)
 
     return jax.shard_map(block, mesh=mesh, in_specs=(row_spec, row_spec) + (P(),) * 7, out_specs=(row_spec, row_spec) + (per_group,) * 7, check_vma=False)

time: 379 us -> 372 us (0.982)
  matrix products: 21.2 us -> 15.8 us
  waiting for transfers between devices: 27.8 us -> 23.5 us
    pallas_call x2 -> x1, Pallas kernels: 33.9 us -> 28.2 us  [finish(): pl.pallas_call(finish_kernel, grid=(steps,), in_specs=[pl.BlockSpec((seq,...]
    all_to_all x2, waiting for transfers between devices: 22 us -> 17.8 us  [exchange(): lax.all_to_all(a, 'cp', 0, 0, tiled=True).reshape(heads, 2, *a.shape[1:])]
    pallas_call x3, Pallas kernels: 164 us -> 168 us  [ring_gather(): pl.pallas_call(functools.partial(ring_kernel, side, counts, make, len(giv...]
    unnamed x25 -> x27, local copies, waits for them, and re-layouts: 13.3 us -> 13.7 us
where the time goes in v3:
time: 372 us; the launch traced here: 371 us
  Pallas kernels  272 us (73%)
  waiting for transfers between devices  23.5 us (6%)
  local copies, waits for them, and re-layouts  22.3 us (6%)
  matrix products  15.8 us (4%)
  between operations  14.1 us (4%)
  other arithmetic  14 us (4%)
  starting transfers between devices  9.88 us (3%)
    pallas_call x3, Pallas kernels, ring_gather(): pl.pallas_call(functools.partial(ring_kernel, side, counts, make, len(giv...  168 us
    pallas_call x1, Pallas kernels, attention(): pl.pallas_call(functools.partial(attn_kernel, scale, shard, half, nope, r...  51.3 us
    pallas_call x1, Pallas kernels, finish(): pl.pallas_call(finish_kernel, grid=(steps,), in_specs=[pl.BlockSpec((seq,...  28.2 us
    all_to_all x2, waiting for transfers between devices, exchange(): lax.all_to_all(a, 'cp', 0, 0, tiled=True).reshape(heads, 2, *a.shape[1:])  17.8 us
    unnamed x27, local copies, waits for them, and re-layouts  13.7 us
    pallas_call x2, Pallas kernels, head_grads(): pl.pallas_call(kernel, grid_spec=pltpu.PrefetchScalarGridSpec(num_scalar_...  13.2 us
    add x4, other arithmetic, summed(): return keep + lax.ppermute(give, 'cp', siblings)  8.3 us
    all_to_all x2, starting transfers between devices, exchange(): lax.all_to_all(a, 'cp', 0, 0, tiled=True).reshape(heads, 2, *a.shape[1:])  7.82 us
  transfers between devices with their start and end apart: 9, of which 4 were waited for; matrix products, arithmetic and copies ran while one was open for 11% of the time, Pallas kernels for 56%

profile of v3, /device:TPU:97, one launch (start us, length us, event | category | flops | bytes accessed | tf_op | source)
XLA Modules:
  0.0 371.4 jit_solution(804834316117022321)
XLA Ops:
  7.3 63.6 %shard_map.178 = (bf16[32,128,2048]{2,1,0:T(8,128)(2,1)}, bf16[32,64,128]{2,1,0:T(8,128)(2,1)}) custom-call(bf16[128,2048]{1,0:T(8,128)(2,1)} %refs_0_.1, bf16[16,128,2048]{2,1,0:T(8,128)(2,1)} %refs_1_.1, bf16[128,2048]{1,0:T(8,128)(2,1)} %refs_2_.1), custom_call_target="tpu_custom_call" | custom-call | flops 40000000000 | tf_op jit(solution)/shard_map/pallas_call | solution.py:409
  71.6 2.1 constant_dynamic-slice_fusion
  75.7 51.3 %shard_map.179 = (bf16[2048,384]{1,0:T(8,128)(2,1)}, bf16[32,160,128]{2,1,0:T(8,128)(2,1)}, f32[2048,384]{1,0:T(8,128)}, f32[2048,384]{1,0:T(8,128)}, bf16[4096,512]{1,0:T(8,128)(2,1)}) custom-call(s32[2]{0:T(128)} %pad_add_fusion.place_ref, bf16[4096,2048]{1,0:T(8,128)(2,1)} %bitcast.54, f32[8,128]{1,0:T(8,128)} %constant.58.clone.far_ref, ...), custom_call_target="tpu_custom_call" | custom-call | flops 27917287424 | bytes 16777216 | tf_op jit(solution)/shard_map/pallas_call | solution.py:233
  127.0 6.9 %shard_map.180 = (f32[96,2048]{1,0:T(8,128)}, f32[96,2048]{1,0:T(8,128)}) custom-call(s32[1]{0:T(128)} %bitcast.core_ref, bf16[32,2,64,2048]{3,2,1,0:T(8,128)(2,1)} %bitcast.55, bf16[2048,384]{1,0:T(8,128)(2,1)} %get-tuple-element.47.odq_ref), custom_call_target="tpu_custom_call" | custom-call | flops 1610612736 | bytes 8388608 | tf_op jit(solution)/shard_map/pallas_call | solution.py:489
  134.1 2.6 collective-permute-done.3
  136.7 2.1 add.70
  139.0 6.2 %shard_map.181 = (f32[64,2048]{1,0:T(8,128)}, f32[64,2048]{1,0:T(8,128)}) custom-call(s32[1]{0:T(128)} %bitcast.core_ref, bf16[32,2,64,2048]{3,2,1,0:T(8,128)(2,1)} %bitcast.60, bf16[2048,384]{1,0:T(8,128)(2,1)} %get-tuple-element.47.odq_ref), custom_call_target="tpu_custom_call" | custom-call | flops 1073741824 | bytes 8388608 | tf_op jit(solution)/shard_map/pallas_call | solution.py:489
  145.6 1.7 collective-permute-done.1
  147.4 2.2 add.60
  150.0 3.8 %all-to-all-start = ((bf16[32,160,128]{2,1,0:T(8,128)(2,1)}), bf16[32,160,128]{2,1,0:T(8,128)(2,1)}, u32[]{:S(2)}, u32[]{:S(2)}) async-start(bf16[32,160,128]{2,1,0:T(8,128)(2,1)} %get-tuple-element.50), calls=%async_computation | async-start | bytes 2621440 | tf_op jit(solution)/shard_map/all_to_all | solution.py:611
  155.7 3.3 add.59
  161.4 17.8 %all-to-all-done = bf16[32,160,128]{2,1,0:T(8,128)(2,1)} async-done(((bf16[32,160,128]{2,1,0:T(8,128)(2,1)}), bf16[32,160,128]{2,1,0:T(8,128)(2,1)}, u32[]{:S(2)}, u32[]{:S(2)}) %all-to-all-start) | async-done | bytes 1310752 | tf_op jit(solution)/shard_map/all_to_all | solution.py:611
  179.2 3.4 shard_map.182
  184.8 1.5 fusion.30
  186.5 7.5 %convolution_bitcast_fusion.1 = f32[128,2048]{1,0:T(8,128)} fusion(bf16[16,128,192]{2,1,0:T(8,128)(2,1)S(1)} %bitcast.64, bf16[2048,16,192]{0,2,1:T(8,128)(2,1)} %param.13), kind=kOutput, calls=%fused_computation.1 | convolution fusion | flops 1610612736 | bytes 14417920 | tf_op jit(solution)/shard_map/hte,dhe->td/dot_general | solution.py:632
  194.1 2.1 fusion
  196.1 4.1 %all-to-all-start.1 = ((bf16[32,64,256]{2,1,0:T(8,128)(2,1)}), bf16[32,64,256]{2,1,0:T(8,128)(2,1)}, u32[]{:S(2)}, u32[]{:S(2)}) async-start(bf16[32,64,256]{2,1,0:T(8,128)(2,1)} %bitcast.17), calls=%async_computation.1 | async-start | bytes 2097152 | tf_op jit(solution)/shard_map/all_to_all | solution.py:611
  200.9 41.4 %shard_map.183 = f32[32,32,128]{2,1,0:T(8,128)} custom-call(f32[32,32,128]{2,1,0:T(8,128)} %reshape.95.refs_0_), custom_call_target="tpu_custom_call" | custom-call | flops 40000000000 | tf_op jit(solution)/shard_map/pallas_call | solution.py:409
  243.9 2.6 fusion.5
  246.5 1.9 multiply_reduce_fusion
  252.5 63.2 %shard_map.184 = (bf16[32,576,128]{2,1,0:T(8,128)(2,1)}, f32[32,32,2048]{2,1,0:T(8,128)}, f32[32,8,128]{2,1,0:T(8,128)}) custom-call(bf16[576,128]{1,0:T(8,128)(2,1)} %maximum_bitcast_fusion.refs_0_, f32[32,2048]{1,0:T(8,128)} %add.61.refs_1_, f32[8,128]{1,0:T(8,128)} %pad.4.refs_2_), custom_call_target="tpu_custom_call" | custom-call | flops 40000000000 | tf_op jit(solution)/shard_map/pallas_call | solution.py:409
  316.6 7.7 %shard_map.186 = (f32[512,16,128]{2,1,0:T(8,128)}, f32[512,16,128]{2,1,0:T(8,128)}) custom-call(f32[16,2,32,2048]{3,2,1,0:T(8,128)} %bitcast.61), custom_call_target="tpu_custom_call" | custom-call | flops 1000000000 | bytes 16777216 | tf_op jit(solution)/shard_map/pallas_call | solution.py:565
  324.9 28.2 %shard_map.185 = (f32[2048,512]{1,0:T(8,128)}, f32[64,2048]{1,0:T(8,128)}, f32[3072,2048]{1,0:T(8,128)}) custom-call(bf16[4096,2048]{1,0:T(8,128)(2,1)} %bitcast.56, bf16[32,576,128]{2,1,0:T(8,128)(2,1)} %get-tuple-element.68.low_ref, f32[3072,2048]{1,0:T(8,128)} %all-gather.6.cloned.1.call-done.g_ref), custom_call_target="tpu_custom_call" | custom-call | flops 9663676416 | bytes 67108864 | tf_op jit(solution)/shard_map/pallas_call | solution.py:545
  353.1 11.8 %copy.70 = f32[16,128,2048]{2,1,0:T(8,128)} copy(f32[16,128,2048]{2,1,0:T(8,128)} %bitcast.59) | data formatting | bytes 33554432
  (71 shorter events, 18.5 us)
Async XLA Ops:
  7.2 63.8 %copy-start.8 = (bf16[512]{0:T(512)(128)(2,1)S(1)}, bf16[512]{0:T(512)(128)(2,1)}, u32[]{:S(2)}) copy-start(bf16[512]{0:T(512)(128)(2,1)} %param.15) | copy-start | bytes 3076
  7.2 131.8 %all-gather.4.cloned.1.call-start = ((), (), s32[]{:S(2)}) async-start(), calls=%async_computation.2 | async-start | bytes 17301504 | tf_op jit(solution)/shard_map/all_gather | solution.py:588
  70.9 254.0 %all-gather.6.cloned.1.call-start = ((), (), s32[]{:S(2)}) async-start(), calls=%async_computation.3 | async-start | bytes 25952256 | tf_op jit(solution)/shard_map/all_gather | solution.py:588
  133.9 2.8 collective-permute-start.3
  138.9 214.2 %all-gather.8.cloned.1.call-start = ((), (), s32[]{:S(2)}) async-start(), calls=%async_computation.4 | async-start | bytes 17301504 | tf_op jit(solution)/shard_map/all_gather | solution.py:588
  145.2 2.1 collective-permute-start.1
  147.4 6.4 %copy-start = (bf16[2048,512]{1,0:T(8,128)(2,1)S(1)}, bf16[2048,512]{1,0:T(8,128)(2,1)}, u32[]{:S(2)}) copy-start(bf16[2048,512]{1,0:T(8,128)(2,1)} %w_ref.1) | copy-start | bytes 6291460
  147.4 6.5 %copy-start.3 = (bf16[128,2048]{1,0:T(8,128)(2,1)S(1)}, bf16[128,2048]{1,0:T(8,128)(2,1)}, u32[]{:S(2)}) copy-start(bf16[128,2048]{1,0:T(8,128)(2,1)} %refs_2_.1) | copy-start | bytes 1572868
  149.6 6.1 %collective-permute-start = (f32[2048,384]{1,0:T(8,128)}, f32[2048,384]{1,0:T(8,128)}, u32[]{:S(2)}, u32[]{:S(2)}) collective-permute-start(f32[2048,384]{1,0:T(8,128)} %get-tuple-element.46), channel_id=1, source_target_pairs={{0,1},{1,0},{2,3},{3,2},{4,5},{5,4},{6,7},{7,6},{8,9},{9,8},{10,11... | collective-permute-start | bytes 9437192 | tf_op jit(solution)/shard_map/ppermute | solution.py:591
  150.0 29.1 %all-to-all-start = ((bf16[32,160,128]{2,1,0:T(8,128)(2,1)}), bf16[32,160,128]{2,1,0:T(8,128)(2,1)}, u32[]{:S(2)}, u32[]{:S(2)}) async-start(bf16[32,160,128]{2,1,0:T(8,128)(2,1)} %get-tuple-element.50), calls=%async_computation | async-start | bytes 2621440 | tf_op jit(solution)/shard_map/all_to_all | solution.py:611
  182.6 17.6 %collective-permute-start.2 = (f32[32,2048]{1,0:T(8,128)}, f32[32,2048]{1,0:T(8,128)S(1)}, u32[]{:S(2)}, u32[]{:S(2)}) collective-permute-start(f32[32,2048]{1,0:T(8,128)} %get-tuple-element.58), channel_id=1, source_target_pairs={{0,1},{1,0},{2,3},{3,2},{4,5},{5,4},{6,7},{7,6},{8,9},{9,8},{10,11... | collective-permute-start | bytes 786440 | tf_op jit(solution)/shard_map/ppermute | solution.py:591
  184.7 9.3 %slice-start = ((s8[8388608]{0:T(1024)(128)(4,1)}), s8[4194304]{0:T(1024)(128)(4,1)S(1)}, s32[]{:S(2)}) async-start(s8[8388608]{0:T(1024)(128)(4,1)} %bitcast.57), calls=%async_computation.5 | async-start | bytes 8388608
  186.5 7.6 %slice-start.1 = ((s8[8388608]{0:T(1024)(128)(4,1)}), s8[4194304]{0:T(1024)(128)(4,1)S(1)}, s32[]{:S(2)}) async-start(s8[8388608]{0:T(1024)(128)(4,1)} %bitcast.57), calls=%async_computation.6 | async-start | bytes 8388608
  196.1 4.1 %copy-start.4 = (f32[32,2048]{1,0:T(8,128)S(1)}, f32[32,2048]{1,0:T(8,128)}, u32[]{:S(2)}) copy-start(f32[32,2048]{1,0:T(8,128)} %get-tuple-element.57) | copy-start | bytes 786436
  196.1 46.2 %all-to-all-start.1 = ((bf16[32,64,256]{2,1,0:T(8,128)(2,1)}), bf16[32,64,256]{2,1,0:T(8,128)(2,1)}, u32[]{:S(2)}, u32[]{:S(2)}) async-start(bf16[32,64,256]{2,1,0:T(8,128)(2,1)} %bitcast.17), calls=%async_computation.1 | async-start | bytes 2097152 | tf_op jit(solution)/shard_map/all_to_all | solution.py:611
  243.7 2.8 copy-start.7
  243.8 2.8 copy-start.6
  246.5 2.9 copy-start.5
  248.4 1.7 copy-start.1
  249.4 1.5 copy-start.2
Sparse Core Ops, SparseCore 0:
  71.0 66.3 all-gather.3
  139.5 117.1 all-gather.5
  259.3 78.8 all-gather.7

commit v4 on v3

--- a/solution.py
+++ b/solution.py
@@ -247,13 +247,15 @@
 
 
 def ring_kernel(side, counts, make, n_given, n_made, *refs):
-    n_ring, n_each, n_same = counts
+    n_ring, n_each, _ = counts
     total = sum(counts)
     given = refs[:n_given]
-    srcs, outs = refs[n_given:n_given + total - n_made], refs[n_given + total - n_made:n_given + 2 * total - n_made]
-    send_sem, recv_sem, own_sem, *rest = refs[n_given + 2 * total - n_made:]
+    srcs, outs = refs[n_given:n_given + total], refs[n_given + total:n_given + 2 * total + n_made]
+    send_sem, recv_sem, own_sem, *rest = refs[n_given + 2 * total + n_made:]
     direct_sem, made = rest[:2], rest[2:]
-    srcs = [*srcs, *made[:n_made]]
+    sent_to = [(srcs[k], outs[k], k < n_ring + n_each) for k in range(n_ring, total)]
+    if make:
+        sent_to.append((made[0], outs[total], True))
     n_dev = 2 * side * side
     me = lax.axis_index("cp")
     pos = ((me // 2) % side, me // (2 * side))
@@ -266,7 +268,7 @@
         return at(second, first) if color else at(first, second)
 
     sibling = me + 1 - 2 * (me % 2)
-    direct = n_each + n_same > 0
+    direct = len(sent_to) > 0
     neighbours = [shifted(color, d, 0) for color in range(2) for d in (1, -1)]
     barrier = pltpu.get_barrier_semaphore()
 
@@ -311,26 +313,28 @@
             ref = part(outs[k].at[block], color, *piece)
             copy(ref, ref, sems(k, color, event), sibling).wait_recv()
 
-    own = [pltpu.make_async_copy(srcs[k].at[me] if n_ring <= k < n_ring + n_each else srcs[k], outs[k].at[me], own_sem.at[k]) for k in range(total)]
+    local = lambda src, dst, k: pltpu.make_async_copy(src, dst, own_sem.at[k])
+    own = [local(srcs[k], outs[k].at[me], k) for k in range(n_ring)]
+    late = [local(src.at[me] if each else src, dst.at[me], n_ring + k) for k, (src, dst, each) in enumerate(sent_to)]
+    late += [local(made[k], outs[total + k], total + k) for k in range(1, n_made)]
 
     def straight(d):
-        for k in range(n_ring, total):
-            src = srcs[k].at[me ^ d] if k < n_ring + n_each else srcs[k]
-            yield copy(src, outs[k].at[me], [s.at[k - n_ring, d] for s in direct_sem], me ^ d)
+        for k, (src, dst, each) in enumerate(sent_to):
+            yield copy(src.at[me ^ d] if each else src, dst.at[me], [s.at[k, d] for s in direct_sem], me ^ d)
 
     def start_direct():
-        for c in own[n_ring:]:
+        for c in late:
             c.start()
         if direct:
             others(lambda d: [c.start() for c in straight(d)])
 
     def wait_all():
-        for c in own:
+        for c in own + late:
             c.wait()
         if direct:
             others(lambda d: [c.wait() for c in straight(d)])
 
-    for c in own[:n_ring]:
+    for c in own:
         c.start()
     if not make:
         start_direct()
@@ -396,35 +400,38 @@
     wait_all()
 
 
-def ring_gather(n_dev, cid, ring, each=(), same=(), make=None, given=(), scratch=()):
+def ring_gather(n_dev, cid, ring, each=(), same=(), make=None, given=(), made=(), scratch=()):
     side = round((n_dev // 2) ** 0.5)
     sent = [*ring, *each, *same]
-    n_made = 1 if make else 0
+    n_made = len(made)
     shapes = [struct(a.shape if len(ring) <= k < len(ring) + len(each) else (n_dev,) + a.shape, a.dtype) for k, a in enumerate(sent)]
-    shapes += [struct(a.shape, a.dtype) for a in scratch[:n_made]]
-    counts = len(ring), len(each) + n_made, len(same)
-    n_direct = sum(counts[1:])
+    shapes += [struct(a.shape, a.dtype) for a in made]
+    counts = len(ring), len(each), len(same)
+    n_direct = sum(counts[1:]) + (1 if make else 0)
     dma = pltpu.SemaphoreType.DMA
     in_vmem, anywhere = pl.BlockSpec(memory_space=pltpu.VMEM), pl.BlockSpec(memory_space=pl.ANY)
     return pl.pallas_call(
         functools.partial(ring_kernel, side, counts, make, len(given), n_made),
         in_specs=[anywhere] * len(given) + [in_vmem] * len(sent), out_specs=[anywhere] * len(shapes), out_shape=shapes,
-        scratch_shapes=[dma((max(len(ring), 1), 2, EVENTS))] * 2 + [dma((len(shapes),))] + [dma((max(n_direct, 1), n_dev))] * 2 + list(scratch),
+        scratch_shapes=[dma((max(len(ring), 1), 2, EVENTS))] * 2 + [dma((len(shapes),))] + [dma((max(n_direct, 1), n_dev))] * 2 + [*made, *scratch],
         compiler_params=compiler_params(collective_id=cid, has_side_effects=True),
         cost_estimate=cost(4e10),
     )(*given, *sent)
 
 
-def make_d_out(gy_ref, w_ref, blocks_ref, gy_vmem, w_vmem, sems):
-    reads = [pltpu.make_async_copy(src, dst, sems.at[k]) for k, (src, dst) in enumerate(((gy_ref, gy_vmem), (w_ref, w_vmem)))]
+def make_early(gy_ref, w_ref, uk_ref, uv_ref, blocks_ref, uk_head_ref, uv_head_ref, *rest):
+    *vmem, sems = rest
+    reads = [pltpu.make_async_copy(src, dst, sems.at[k]) for k, (src, dst) in enumerate(zip((gy_ref, w_ref, uk_ref, uv_ref), vmem))]
     for c in reads:
         c.start()
+    gy_vmem, w_vmem, uk_vmem, uv_vmem = vmem
 
     def compute():
         for c in reads:
             c.wait()
         heads, v_dim = w_ref.shape[:2]
         half = blocks_ref.shape[1]
+        head = lax.axis_index("cp") // 2
 
         def two_heads(b, _):
             w = w_vmem[pl.ds(2 * b, 2)].reshape(2 * v_dim, -1)
@@ -435,6 +442,15 @@
             return 0
 
         lax.fori_loop(0, heads // 2, two_heads, 0)
+
+        def pick(b, _):
+            r = at_block(b, LANES)
+            for src, dst in ((uk_vmem, uk_head_ref), (uv_vmem, uv_head_ref)):
+                w = src[r].astype(F32)
+                dst[r, :] = jnp.sum(jnp.where(lax.broadcasted_iota(jnp.int32, w.shape, 1) == head, w, 0.0), axis=1).astype(BF16)
+            return 0
+
+        lax.fori_loop(0, uk_head_ref.shape[0] // LANES, pick, 0)
 
     return compute
 
@@ -591,14 +607,12 @@
             return keep + lax.ppermute(give, 'cp', siblings)
 
         packed = lambda *shape: pltpu.VMEM(shape, BF16)
-        scratch = packed(n_dev, half, v_dim), packed(*gy_loc.shape), packed(*w_o.shape), pltpu.SemaphoreType.DMA((2,))
-        x_all, d_out = ring_gather(n_dev, 1, [x_loc], make=make_d_out, given=[gy_loc, w_o], scratch=scratch)
+        given = gy_loc, w_o, w_uk, w_uv
+        x_all, d_out, uk, uv = ring_gather(n_dev, 1, [x_loc], make=make_early, given=given, made=(packed(n_dev, half, v_dim), packed(rank, nope), packed(rank, v_dim)),
+                                           scratch=[*(packed(*a.shape) for a in given), pltpu.SemaphoreType.DMA((len(given),))])
         x_all, d_out = x_all.reshape(seq, d_model), d_out.reshape(seq // 2, v_dim)
         gy_all = gather(lax.optimization_barrier((gy_loc, x_all))[0])
 
-        pick = lambda a, axis: lax.dynamic_index_in_dim(a, head, axis, False)
-        uk, uv = pick(w_uk, 1), pick(w_uv, 1)
-        w_uk, w_uv, _ = lax.optimization_barrier((w_uk, w_uv, x_all))
 
         def table(positions):
             return np.concatenate([t for t in rope_tables(positions.astype(np.float32), rope, np) for _ in range(LANES // rope)], axis=1)
@@ -610,8 +624,8 @@
         def exchange(a):
             return lax.all_to_all(a, 'cp', 0, 0, tiled=True).reshape(heads, 2, *a.shape[1:])
 
-        got_odq = exchange(sent)
         q_keep, q_give = head_grads(functools.partial(query_grads_kernel, qk_dim), core, x_all, odq, n_dev, half, qk_dim)
+        got_odq = exchange(lax.optimization_barrier((sent, q_keep))[0])
         q_my = summed(q_keep, q_give)
         gwq = gather(q_my)
 

time: 372 us -> 372 us (level)
    unnamed x27 -> x25, local copies, waits for them, and re-layouts: 13.7 us -> 12.3 us
  transfers between devices with their start and end apart: 9 -> 9, of which waited for: 4 -> 5; matrix products, arithmetic and copies ran while one was open for 11% -> 10% of each run, Pallas kernels for 56% -> 56%
where the time goes in v4:
time: 372 us; the launch traced here: 371 us
  Pallas kernels  272 us (73%)
  waiting for transfers between devices  27 us (7%)
  local copies, waits for them, and re-layouts  18.9 us (5%)
  matrix products  15.8 us (4%)
  between operations  14.1 us (4%)
  other arithmetic  13.9 us (4%)
  starting transfers between devices  10 us (3%)
    pallas_call x3, Pallas kernels, ring_gather(): pl.pallas_call(functools.partial(ring_kernel, side, counts, make, len(giv...  168 us
    pallas_call x1, Pallas kernels, attention(): pl.pallas_call(functools.partial(attn_kernel, scale, shard, half, nope, r...  50.9 us
    pallas_call x1, Pallas kernels, finish(): pl.pallas_call(finish_kernel, grid=(steps,), in_specs=[pl.BlockSpec((seq,...  28.2 us
    all_to_all x2, waiting for transfers between devices, exchange(): lax.all_to_all(a, 'cp', 0, 0, tiled=True).reshape(heads, 2, *a.shape[1:])  19.4 us
    pallas_call x2, Pallas kernels, head_grads(): pl.pallas_call(kernel, grid_spec=pltpu.PrefetchScalarGridSpec(num_scalar_...  13.4 us
    unnamed x25, local copies, waits for them, and re-layouts  12.3 us
    add x4, other arithmetic, summed(): return keep + lax.ppermute(give, 'cp', siblings)  8.29 us
    all_to_all x2, starting transfers between devices, exchange(): lax.all_to_all(a, 'cp', 0, 0, tiled=True).reshape(heads, 2, *a.shape[1:])  8.28 us
  transfers between devices with their start and end apart: 9, of which 5 were waited for; matrix products, arithmetic and copies ran while one was open for 10% of the time, Pallas kernels for 56%

profile of v4, /device:TPU:97, one launch (start us, length us, event | category | flops | bytes accessed | tf_op | source)
XLA Modules:
  0.0 371.4 jit_solution(5618553607974642757)
XLA Ops:
  7.3 63.6 %shard_map.178 = (bf16[32,128,2048]{2,1,0:T(8,128)(2,1)}, bf16[32,64,128]{2,1,0:T(8,128)(2,1)}, bf16[512,128]{1,0:T(8,128)(2,1)}, bf16[512,128]{1,0:T(8,128)(2,1)}) custom-call(bf16[128,2048]{1,0:T(8,128)(2,1)} %refs_0_.1, bf16[16,128,2048]{2,1,0:T(8,128)(2,1)} %refs_1_.1, bf16[512,16,128]{2,1,0:T(8,128)(2,1)} %refs_2_.1, bf16[512,16,128]{2,1,0:T(8,128)(2,1)} %refs_3_.1, ...), custom_call_target="tpu_custom_call" | custom-call | flops 40000000000 | tf_op jit(solution)/shard_map/pallas_call | solution.py:413
  72.2 50.9 %shard_map.179 = (bf16[2048,384]{1,0:T(8,128)(2,1)}, bf16[32,160,128]{2,1,0:T(8,128)(2,1)}, f32[2048,384]{1,0:T(8,128)}, f32[2048,384]{1,0:T(8,128)}, bf16[4096,512]{1,0:T(8,128)(2,1)}) custom-call(s32[2]{0:T(128)} %pad_add_fusion.place_ref, bf16[4096,2048]{1,0:T(8,128)(2,1)} %bitcast.48, f32[8,128]{1,0:T(8,128)} %constant.51.clone.far_ref, ...), custom_call_target="tpu_custom_call" | custom-call | flops 27917287424 | bytes 16777216 | tf_op jit(solution)/shard_map/pallas_call | solution.py:233
  123.1 7.2 %shard_map.180 = (f32[96,2048]{1,0:T(8,128)}, f32[96,2048]{1,0:T(8,128)}) custom-call(s32[1]{0:T(128)} %bitcast.core_ref, bf16[32,2,64,2048]{3,2,1,0:T(8,128)(2,1)} %bitcast.49, bf16[2048,384]{1,0:T(8,128)(2,1)} %get-tuple-element.50.odq_ref), custom_call_target="tpu_custom_call" | custom-call | flops 1610612736 | bytes 8388608 | tf_op jit(solution)/shard_map/pallas_call | solution.py:505
  130.4 2.8 collective-permute-done.3
  133.1 2.1 add.64
  135.4 2.0 all-gather.4.cloned.1.call-done
  137.5 6.2 %shard_map.181 = (f32[64,2048]{1,0:T(8,128)}, f32[64,2048]{1,0:T(8,128)}) custom-call(s32[1]{0:T(128)} %bitcast.core_ref, bf16[32,2,64,2048]{3,2,1,0:T(8,128)(2,1)} %bitcast.54, bf16[2048,384]{1,0:T(8,128)(2,1)} %get-tuple-element.50.odq_ref), custom_call_target="tpu_custom_call" | custom-call | flops 1073741824 | bytes 8388608 | tf_op jit(solution)/shard_map/pallas_call | solution.py:505
  143.9 1.9 collective-permute-done.1
  145.8 2.1 add.54
  148.3 4.2 %all-to-all-start = ((bf16[32,160,128]{2,1,0:T(8,128)(2,1)}), bf16[32,160,128]{2,1,0:T(8,128)(2,1)}, u32[]{:S(2)}, u32[]{:S(2)}) async-start(bf16[32,160,128]{2,1,0:T(8,128)(2,1)} %get-tuple-element.54), calls=%async_computation | async-start | bytes 2621440 | tf_op jit(solution)/shard_map/all_to_all | solution.py:625
  154.1 3.3 add.53
  159.8 19.4 %all-to-all-done = bf16[32,160,128]{2,1,0:T(8,128)(2,1)} async-done(((bf16[32,160,128]{2,1,0:T(8,128)(2,1)}), bf16[32,160,128]{2,1,0:T(8,128)(2,1)}, u32[]{:S(2)}, u32[]{:S(2)}) %all-to-all-start) | async-done | bytes 1310752 | tf_op jit(solution)/shard_map/all_to_all | solution.py:625
  179.1 3.4 shard_map.182
  184.8 1.5 fusion.30
  186.6 7.5 %convolution_bitcast_fusion.1 = f32[128,2048]{1,0:T(8,128)} fusion(bf16[16,128,192]{2,1,0:T(8,128)(2,1)S(1)} %bitcast.58, bf16[2048,16,192]{0,2,1:T(8,128)(2,1)} %param.13), kind=kOutput, calls=%fused_computation.1 | convolution fusion | flops 1610612736 | bytes 14417920 | tf_op jit(solution)/shard_map/hte,dhe->td/dot_general | solution.py:646
  194.1 2.1 fusion
  196.2 4.0 %all-to-all-start.1 = ((bf16[32,64,256]{2,1,0:T(8,128)(2,1)}), bf16[32,64,256]{2,1,0:T(8,128)(2,1)}, u32[]{:S(2)}, u32[]{:S(2)}) async-start(bf16[32,64,256]{2,1,0:T(8,128)(2,1)} %bitcast.15), calls=%async_computation.1 | async-start | bytes 2097152 | tf_op jit(solution)/shard_map/all_to_all | solution.py:625
  201.0 41.4 %shard_map.183 = f32[32,32,128]{2,1,0:T(8,128)} custom-call(f32[32,32,128]{2,1,0:T(8,128)} %reshape.95.refs_0_), custom_call_target="tpu_custom_call" | custom-call | flops 40000000000 | tf_op jit(solution)/shard_map/pallas_call | solution.py:413
  244.0 2.6 fusion.5
  246.6 1.9 multiply_reduce_fusion
  252.6 63.1 %shard_map.184 = (bf16[32,576,128]{2,1,0:T(8,128)(2,1)}, f32[32,32,2048]{2,1,0:T(8,128)}, f32[32,8,128]{2,1,0:T(8,128)}) custom-call(bf16[576,128]{1,0:T(8,128)(2,1)} %maximum_bitcast_fusion.refs_0_, f32[32,2048]{1,0:T(8,128)} %add.55.refs_1_, f32[8,128]{1,0:T(8,128)} %pad.4.refs_2_), custom_call_target="tpu_custom_call" | custom-call | flops 40000000000 | tf_op jit(solution)/shard_map/pallas_call | solution.py:413
  316.6 7.7 %shard_map.186 = (f32[512,16,128]{2,1,0:T(8,128)}, f32[512,16,128]{2,1,0:T(8,128)}) custom-call(f32[16,2,32,2048]{3,2,1,0:T(8,128)} %bitcast.55), custom_call_target="tpu_custom_call" | custom-call | flops 1000000000 | bytes 16777216 | tf_op jit(solution)/shard_map/pallas_call | solution.py:581
  324.9 28.2 %shard_map.185 = (f32[2048,512]{1,0:T(8,128)}, f32[64,2048]{1,0:T(8,128)}, f32[3072,2048]{1,0:T(8,128)}) custom-call(bf16[4096,2048]{1,0:T(8,128)(2,1)} %bitcast.50, bf16[32,576,128]{2,1,0:T(8,128)(2,1)} %get-tuple-element.70.low_ref, f32[3072,2048]{1,0:T(8,128)} %all-gather.6.cloned.1.call-done.g_ref), custom_call_target="tpu_custom_call" | custom-call | flops 9663676416 | bytes 67108864 | tf_op jit(solution)/shard_map/pallas_call | solution.py:561
  353.1 11.8 %copy.60 = f32[16,128,2048]{2,1,0:T(8,128)} copy(f32[16,128,2048]{2,1,0:T(8,128)} %bitcast.53) | data formatting | bytes 33554432
  (68 shorter events, 16.4 us)
Async XLA Ops:
  7.2 63.9 %copy-start.7 = (bf16[512]{0:T(512)(128)(2,1)S(1)}, bf16[512]{0:T(512)(128)(2,1)}, u32[]{:S(2)}) copy-start(bf16[512]{0:T(512)(128)(2,1)} %param.15) | copy-start | bytes 3076
  7.2 130.3 %all-gather.4.cloned.1.call-start = ((), (), s32[]{:S(2)}) async-start(), calls=%async_computation.2 | async-start | bytes 17301504 | tf_op jit(solution)/shard_map/all_gather | solution.py:604
  71.0 253.9 %all-gather.6.cloned.1.call-start = ((), (), s32[]{:S(2)}) async-start(), calls=%async_computation.3 | async-start | bytes 25952256 | tf_op jit(solution)/shard_map/all_gather | solution.py:604
  130.4 2.8 collective-permute-start.3
  135.3 217.7 %all-gather.8.cloned.1.call-start = ((), (), s32[]{:S(2)}) async-start(), calls=%async_computation.4 | async-start | bytes 17301504 | tf_op jit(solution)/shard_map/all_gather | solution.py:604
  143.7 2.1 collective-permute-start.1
  145.8 6.8 %copy-start = (bf16[2048,512]{1,0:T(8,128)(2,1)S(1)}, bf16[2048,512]{1,0:T(8,128)(2,1)}, u32[]{:S(2)}) copy-start(bf16[2048,512]{1,0:T(8,128)(2,1)} %w_ref.1) | copy-start | bytes 6291460
  145.8 6.8 %copy-start.3 = (bf16[128,2048]{1,0:T(8,128)(2,1)S(1)}, bf16[128,2048]{1,0:T(8,128)(2,1)}, u32[]{:S(2)}) copy-start(bf16[128,2048]{1,0:T(8,128)(2,1)} %refs_4_.1) | copy-start | bytes 1572868
  148.0 6.1 %collective-permute-start = (f32[2048,384]{1,0:T(8,128)}, f32[2048,384]{1,0:T(8,128)}, u32[]{:S(2)}, u32[]{:S(2)}) collective-permute-start(f32[2048,384]{1,0:T(8,128)} %get-tuple-element.49), channel_id=1, source_target_pairs={{0,1},{1,0},{2,3},{3,2},{4,5},{5,4},{6,7},{7,6},{8,9},{9,8},{10,11... | collective-permute-start | bytes 9437192 | tf_op jit(solution)/shard_map/ppermute | solution.py:607
  148.3 30.8 %all-to-all-start = ((bf16[32,160,128]{2,1,0:T(8,128)(2,1)}), bf16[32,160,128]{2,1,0:T(8,128)(2,1)}, u32[]{:S(2)}, u32[]{:S(2)}) async-start(bf16[32,160,128]{2,1,0:T(8,128)(2,1)} %get-tuple-element.54), calls=%async_computation | async-start | bytes 2621440 | tf_op jit(solution)/shard_map/all_to_all | solution.py:625
  182.6 17.7 %collective-permute-start.2 = (f32[32,2048]{1,0:T(8,128)}, f32[32,2048]{1,0:T(8,128)S(1)}, u32[]{:S(2)}, u32[]{:S(2)}) collective-permute-start(f32[32,2048]{1,0:T(8,128)} %get-tuple-element.62), channel_id=1, source_target_pairs={{0,1},{1,0},{2,3},{3,2},{4,5},{5,4},{6,7},{7,6},{8,9},{9,8},{10,11... | collective-permute-start | bytes 786440 | tf_op jit(solution)/shard_map/ppermute | solution.py:607
  184.8 9.3 %slice-start = ((s8[8388608]{0:T(1024)(128)(4,1)}), s8[4194304]{0:T(1024)(128)(4,1)S(1)}, s32[]{:S(2)}) async-start(s8[8388608]{0:T(1024)(128)(4,1)} %bitcast.51), calls=%async_computation.5 | async-start | bytes 8388608
  186.6 7.6 %slice-start.1 = ((s8[8388608]{0:T(1024)(128)(4,1)}), s8[4194304]{0:T(1024)(128)(4,1)S(1)}, s32[]{:S(2)}) async-start(s8[8388608]{0:T(1024)(128)(4,1)} %bitcast.51), calls=%async_computation.6 | async-start | bytes 8388608
  196.2 4.1 %copy-start.4 = (f32[32,2048]{1,0:T(8,128)S(1)}, f32[32,2048]{1,0:T(8,128)}, u32[]{:S(2)}) copy-start(f32[32,2048]{1,0:T(8,128)} %get-tuple-element.61) | copy-start | bytes 786436
  196.2 46.2 %all-to-all-start.1 = ((bf16[32,64,256]{2,1,0:T(8,128)(2,1)}), bf16[32,64,256]{2,1,0:T(8,128)(2,1)}, u32[]{:S(2)}, u32[]{:S(2)}) async-start(bf16[32,64,256]{2,1,0:T(8,128)(2,1)} %bitcast.15), calls=%async_computation.1 | async-start | bytes 2097152 | tf_op jit(solution)/shard_map/all_to_all | solution.py:625
  243.7 2.8 copy-start.6
  243.8 2.8 copy-start.8
  246.6 2.9 copy-start.5
  248.5 1.7 copy-start.1
  249.5 1.5 copy-start.2
Sparse Core Ops, SparseCore 0:
  71.1 66.3 all-gather.3
  139.5 117.0 all-gather.5
  259.3 78.8 all-gather.7

commit v5 on v4

--- a/solution.py
+++ b/solution.py
@@ -639,14 +639,15 @@
         got_kv = exchange(kv_my.reshape(n_dev, half, -1))
         up_keep, up_give = up_grads(core, latent, kv_my, d_model, n_dev, half)
         up_my = summed(up_keep, up_give)
+        dkr_my, _, _ = lax.optimization_barrier((dkr_my, o_my, up_my))
+        got_r, = ring_gather(n_dev, 2, [], [dkr_my])
+        got_odq, got_r = lax.optimization_barrier((got_odq, got_r))
         o_loc, dq_loc, dq_rope = jnp.split(got_odq, [half, 2 * half], axis=2)
         dq_loc = jnp.concatenate([dq_loc, jnp.concatenate([dq_rope[..., :rope], dq_rope[..., rope:]], axis=2)], axis=3)
         o_loc, dq_loc = o_loc.reshape(heads, shard, -1), dq_loc.reshape(heads, shard, -1)
         y_loc = jnp.einsum('htv,hvd->td', o_loc, w_o, preferred_element_type=F32).astype(BF16)
         dx_loc = jnp.einsum('hte,dhe->td', dq_loc, w_q, preferred_element_type=F32)
-        dkr_my, y_loc, dx_loc, _, _ = lax.optimization_barrier((dkr_my, y_loc, dx_loc, o_my, up_my))
-        got_r, = ring_gather(n_dev, 2, [], [dkr_my])
-        got_kv, got_r = lax.optimization_barrier((got_kv, got_r))
+        got_kv, got_r, y_loc, dx_loc = lax.optimization_barrier((got_kv, got_r, y_loc, dx_loc))
         dkr_loc = jnp.sum(got_r.reshape(heads, shard, rope), axis=0)
         dk_loc, dv_loc = jnp.split(got_kv.reshape(heads, shard, -1), [nope], axis=2)
         d_latent = jnp.einsum('htn,chn->tc', dk_loc, w_uk, preferred_element_type=F32) + jnp.einsum('htv,chv->tc', dv_loc, w_uv, preferred_element_type=F32)

time: 372 us -> 379 us (1.019)
  matrix products: 15.8 us -> 19.8 us
    pallas_call x3, Pallas kernels: 168 us -> 172 us  [ring_gather(): pl.pallas_call(functools.partial(ring_kernel, side, counts, make, len(giv...]
    dot_general x1, matrix products: 2.05 us -> 5.92 us  [block(): jnp.einsum('htv,hvd->td', o_loc, w_o, preferred_element_type=F32)]
    unnamed x25 -> x23, local copies, waits for them, and re-layouts: 12.3 us -> 13.6 us
where the time goes in v5:
time: 379 us; the launch traced here: 378 us
  Pallas kernels  275 us (73%)
  waiting for transfers between devices  26.7 us (7%)
  matrix products  19.8 us (5%)
  local copies, waits for them, and re-layouts  19.1 us (5%)
  between operations  14.1 us (4%)
  other arithmetic  13 us (3%)
  starting transfers between devices  10.1 us (3%)
    pallas_call x3, Pallas kernels, ring_gather(): pl.pallas_call(functools.partial(ring_kernel, side, counts, make, len(giv...  172 us
    pallas_call x1, Pallas kernels, attention(): pl.pallas_call(functools.partial(attn_kernel, scale, shard, half, nope, r...  50.9 us
    pallas_call x1, Pallas kernels, finish(): pl.pallas_call(finish_kernel, grid=(steps,), in_specs=[pl.BlockSpec((seq,...  28 us
    all_to_all x2, waiting for transfers between devices, exchange(): lax.all_to_all(a, 'cp', 0, 0, tiled=True).reshape(heads, 2, *a.shape[1:])  19 us
    unnamed x23, local copies, waits for them, and re-layouts  13.6 us
    pallas_call x2, Pallas kernels, head_grads(): pl.pallas_call(kernel, grid_spec=pltpu.PrefetchScalarGridSpec(num_scalar_...  13.4 us
    all_to_all x2, starting transfers between devices, exchange(): lax.all_to_all(a, 'cp', 0, 0, tiled=True).reshape(heads, 2, *a.shape[1:])  8.35 us
    add x4, other arithmetic, summed(): return keep + lax.ppermute(give, 'cp', siblings)  8.28 us
  transfers between devices with their start and end apart: 9, of which 5 were waited for; matrix products, arithmetic and copies ran while one was open for 10% of the time, Pallas kernels for 56%

profile of v5, /device:TPU:97, one launch (start us, length us, event | category | flops | bytes accessed | tf_op | source)
XLA Modules:
  0.0 378.1 jit_solution(3037199469871756812)
XLA Ops:
  7.3 63.6 %shard_map.178 = (bf16[32,128,2048]{2,1,0:T(8,128)(2,1)}, bf16[32,64,128]{2,1,0:T(8,128)(2,1)}, bf16[512,128]{1,0:T(8,128)(2,1)}, bf16[512,128]{1,0:T(8,128)(2,1)}) custom-call(bf16[128,2048]{1,0:T(8,128)(2,1)} %refs_0_.1, bf16[16,128,2048]{2,1,0:T(8,128)(2,1)} %refs_1_.1, bf16[512,16,128]{2,1,0:T(8,128)(2,1)} %refs_2_.1, bf16[512,16,128]{2,1,0:T(8,128)(2,1)} %refs_3_.1, ...), custom_call_target="tpu_custom_call" | custom-call | flops 40000000000 | tf_op jit(solution)/shard_map/pallas_call | solution.py:413
  72.2 50.9 %shard_map.179 = (bf16[2048,384]{1,0:T(8,128)(2,1)}, bf16[32,160,128]{2,1,0:T(8,128)(2,1)}, f32[2048,384]{1,0:T(8,128)}, f32[2048,384]{1,0:T(8,128)}, bf16[4096,512]{1,0:T(8,128)(2,1)}) custom-call(s32[2]{0:T(128)} %pad_add_fusion.place_ref, bf16[4096,2048]{1,0:T(8,128)(2,1)} %bitcast.48, f32[8,128]{1,0:T(8,128)} %constant.51.clone.far_ref, ...), custom_call_target="tpu_custom_call" | custom-call | flops 27917287424 | bytes 16777216 | tf_op jit(solution)/shard_map/pallas_call | solution.py:233
  123.1 7.2 %shard_map.180 = (f32[96,2048]{1,0:T(8,128)}, f32[96,2048]{1,0:T(8,128)}) custom-call(s32[1]{0:T(128)} %bitcast.core_ref, bf16[32,2,64,2048]{3,2,1,0:T(8,128)(2,1)} %bitcast.49, bf16[2048,384]{1,0:T(8,128)(2,1)} %get-tuple-element.51.odq_ref), custom_call_target="tpu_custom_call" | custom-call | flops 1610612736 | bytes 8388608 | tf_op jit(solution)/shard_map/pallas_call | solution.py:505
  130.4 2.8 collective-permute-done.3
  133.1 2.1 add.64
  135.4 2.1 all-gather.4.cloned.1.call-done
  137.5 6.2 %shard_map.181 = (f32[64,2048]{1,0:T(8,128)}, f32[64,2048]{1,0:T(8,128)}) custom-call(s32[1]{0:T(128)} %bitcast.core_ref, bf16[32,2,64,2048]{3,2,1,0:T(8,128)(2,1)} %bitcast.52, bf16[2048,384]{1,0:T(8,128)(2,1)} %get-tuple-element.51.odq_ref), custom_call_target="tpu_custom_call" | custom-call | flops 1073741824 | bytes 8388608 | tf_op jit(solution)/shard_map/pallas_call | solution.py:505
  143.9 1.9 collective-permute-done.1
  145.8 2.1 add.54
  148.3 4.2 %all-to-all-start = ((bf16[32,160,128]{2,1,0:T(8,128)(2,1)}), bf16[32,160,128]{2,1,0:T(8,128)(2,1)}, u32[]{:S(2)}, u32[]{:S(2)}) async-start(bf16[32,160,128]{2,1,0:T(8,128)(2,1)} %get-tuple-element.53), calls=%async_computation | async-start | bytes 2621440 | tf_op jit(solution)/shard_map/all_to_all | solution.py:625
  154.1 3.3 add.53
  157.6 1.5 copy-done
  160.2 19.0 %all-to-all-done = bf16[32,160,128]{2,1,0:T(8,128)(2,1)} async-done(((bf16[32,160,128]{2,1,0:T(8,128)(2,1)}), bf16[32,160,128]{2,1,0:T(8,128)(2,1)}, u32[]{:S(2)}, u32[]{:S(2)}) %all-to-all-start) | async-done | bytes 1310752 | tf_op jit(solution)/shard_map/all_to_all | solution.py:625
  179.1 3.4 shard_map.182
  185.1 4.1 %all-to-all-start.1 = ((bf16[32,64,256]{2,1,0:T(8,128)(2,1)}), bf16[32,64,256]{2,1,0:T(8,128)(2,1)}, u32[]{:S(2)}, u32[]{:S(2)}) async-start(bf16[32,64,256]{2,1,0:T(8,128)(2,1)} %bitcast.10), calls=%async_computation.1 | async-start | bytes 2097152 | tf_op jit(solution)/shard_map/all_to_all | solution.py:625
  189.9 41.8 %shard_map.183 = f32[32,32,128]{2,1,0:T(8,128)} custom-call(f32[32,32,128]{2,1,0:T(8,128)} %reshape.99.refs_0_), custom_call_target="tpu_custom_call" | custom-call | flops 40000000000 | tf_op jit(solution)/shard_map/pallas_call | solution.py:413
  233.0 5.9 %fusion = bf16[128,2048]{1,0:T(8,128)(2,1)} fusion(bf16[16,128,128]{2,1,0:T(8,128)(2,1)S(1)} %bitcast.55, bf16[16,128,2048]{2,1,0:T(8,128)(2,1)} %refs_1_.1), kind=kOutput, calls=%fused_computation.4 | convolution fusion | flops 1074003968 | bytes 9437184 | tf_op jit(solution)/shard_map/htv,hvd->td/dot_general | solution.py:648
  240.4 6.7 %convolution_bitcast_fusion.1 = f32[128,2048]{1,0:T(8,128)S(1)} fusion(bf16[16,128,192]{2,1,0:T(8,128)(2,1)S(1)} %bitcast.56, bf16[2048,16,192]{0,2,1:T(8,128)(2,1)} %param.13), kind=kOutput, calls=%fused_computation.3 | convolution fusion | flops 1610612736 | bytes 14417920 | tf_op jit(solution)/shard_map/hte,dhe->td/dot_general | solution.py:649
  247.7 2.6 fusion.6
  250.4 2.0 multiply_reduce_fusion
  256.0 66.7 %shard_map.184 = (bf16[32,576,128]{2,1,0:T(8,128)(2,1)}, f32[32,32,2048]{2,1,0:T(8,128)}, f32[32,8,128]{2,1,0:T(8,128)}) custom-call(bf16[576,128]{1,0:T(8,128)(2,1)} %maximum_bitcast_fusion.refs_0_, f32[32,2048]{1,0:T(8,128)} %add.55.refs_1_, f32[8,128]{1,0:T(8,128)} %pad.4.refs_2_), custom_call_target="tpu_custom_call" | custom-call | flops 40000000000 | tf_op jit(solution)/shard_map/pallas_call | solution.py:413
  323.7 7.6 %shard_map.186 = (f32[512,16,128]{2,1,0:T(8,128)}, f32[512,16,128]{2,1,0:T(8,128)}) custom-call(f32[16,2,32,2048]{3,2,1,0:T(8,128)} %bitcast.53), custom_call_target="tpu_custom_call" | custom-call | flops 1000000000 | bytes 16777216 | tf_op jit(solution)/shard_map/pallas_call | solution.py:581
  331.8 28.0 %shard_map.185 = (f32[2048,512]{1,0:T(8,128)}, f32[64,2048]{1,0:T(8,128)}, f32[3072,2048]{1,0:T(8,128)}) custom-call(bf16[4096,2048]{1,0:T(8,128)(2,1)} %bitcast.50, bf16[32,576,128]{2,1,0:T(8,128)(2,1)} %get-tuple-element.74.low_ref, f32[3072,2048]{1,0:T(8,128)} %all-gather.6.cloned.1.call-done.g_ref), custom_call_target="tpu_custom_call" | custom-call | flops 9663676416 | bytes 67108864 | tf_op jit(solution)/shard_map/pallas_call | solution.py:561
  359.8 11.8 %copy.60 = f32[16,128,2048]{2,1,0:T(8,128)} copy(f32[16,128,2048]{2,1,0:T(8,128)} %bitcast.51) | data formatting | bytes 33554432
  (65 shorter events, 16.6 us)
Async XLA Ops:
  7.2 63.9 %copy-start.8 = (bf16[512]{0:T(512)(128)(2,1)S(1)}, bf16[512]{0:T(512)(128)(2,1)}, u32[]{:S(2)}) copy-start(bf16[512]{0:T(512)(128)(2,1)} %param.15) | copy-start | bytes 3076
  7.2 130.3 %all-gather.4.cloned.1.call-start = ((), (), s32[]{:S(2)}) async-start(), calls=%async_computation.2 | async-start | bytes 17301504 | tf_op jit(solution)/shard_map/all_gather | solution.py:604
  71.0 260.9 %all-gather.6.cloned.1.call-start = ((), (), s32[]{:S(2)}) async-start(), calls=%async_computation.3 | async-start | bytes 25952256 | tf_op jit(solution)/shard_map/all_gather | solution.py:604
  130.4 2.8 collective-permute-start.3
  135.3 224.5 %all-gather.8.cloned.1.call-start = ((), (), s32[]{:S(2)}) async-start(), calls=%async_computation.4 | async-start | bytes 17301504 | tf_op jit(solution)/shard_map/all_gather | solution.py:604
  143.7 2.1 collective-permute-start.1
  145.8 6.8 %copy-start.1 = (bf16[2048,512]{1,0:T(8,128)(2,1)S(1)}, bf16[2048,512]{1,0:T(8,128)(2,1)}, u32[]{:S(2)}) copy-start(bf16[2048,512]{1,0:T(8,128)(2,1)} %w_ref.1) | copy-start | bytes 6291460
  145.8 6.8 %copy-start.4 = (bf16[128,2048]{1,0:T(8,128)(2,1)S(1)}, bf16[128,2048]{1,0:T(8,128)(2,1)}, u32[]{:S(2)}) copy-start(bf16[128,2048]{1,0:T(8,128)(2,1)} %refs_4_.1) | copy-start | bytes 1572868
  148.0 6.1 %collective-permute-start = (f32[2048,384]{1,0:T(8,128)}, f32[2048,384]{1,0:T(8,128)}, u32[]{:S(2)}, u32[]{:S(2)}) collective-permute-start(f32[2048,384]{1,0:T(8,128)} %get-tuple-element.55), channel_id=1, source_target_pairs={{0,1},{1,0},{2,3},{3,2},{4,5},{5,4},{6,7},{7,6},{8,9},{9,8},{10,11... | collective-permute-start | bytes 9437192 | tf_op jit(solution)/shard_map/ppermute | solution.py:607
  148.3 30.8 %all-to-all-start = ((bf16[32,160,128]{2,1,0:T(8,128)(2,1)}), bf16[32,160,128]{2,1,0:T(8,128)(2,1)}, u32[]{:S(2)}, u32[]{:S(2)}) async-start(bf16[32,160,128]{2,1,0:T(8,128)(2,1)} %get-tuple-element.53), calls=%async_computation | async-start | bytes 2621440 | tf_op jit(solution)/shard_map/all_to_all | solution.py:625
  157.4 1.7 copy-start
  182.6 1.5 slice-start
  182.6 6.6 %collective-permute-start.2 = (f32[32,2048]{1,0:T(8,128)}, f32[32,2048]{1,0:T(8,128)S(1)}, u32[]{:S(2)}, u32[]{:S(2)}) collective-permute-start(f32[32,2048]{1,0:T(8,128)} %get-tuple-element.64), channel_id=1, source_target_pairs={{0,1},{1,0},{2,3},{3,2},{4,5},{5,4},{6,7},{7,6},{8,9},{9,8},{10,11... | collective-permute-start | bytes 786440 | tf_op jit(solution)/shard_map/ppermute | solution.py:607
  184.1 5.1 %copy-start.6 = (f32[32,2048]{1,0:T(8,128)S(1)}, f32[32,2048]{1,0:T(8,128)}, u32[]{:S(2)}) copy-start(f32[32,2048]{1,0:T(8,128)} %get-tuple-element.63) | copy-start | bytes 786436
  185.1 62.1 %all-to-all-start.1 = ((bf16[32,64,256]{2,1,0:T(8,128)(2,1)}), bf16[32,64,256]{2,1,0:T(8,128)(2,1)}, u32[]{:S(2)}, u32[]{:S(2)}) async-start(bf16[32,64,256]{2,1,0:T(8,128)(2,1)} %bitcast.10), calls=%async_computation.1 | async-start | bytes 2097152 | tf_op jit(solution)/shard_map/all_to_all | solution.py:625
  240.4 6.8 %copy-start.3 = (f32[32,32,128]{2,1,0:T(8,128)S(1)}, f32[32,32,128]{2,1,0:T(8,128)}, u32[]{:S(2)}) copy-start(f32[32,32,128]{2,1,0:T(8,128)} %shard_map.183) | copy-start | bytes 1572868
  247.5 2.9 copy-start.7
  247.7 2.7 copy-start.9
  250.4 3.0 copy-start.2
  253.3 1.0 copy-start.5
Sparse Core Ops, SparseCore 0:
  71.1 66.3 all-gather.3
  139.5 117.0 all-gather.5
  259.3 82.5 all-gather.7

commit v6 on v5

--- a/solution.py
+++ b/solution.py
@@ -537,7 +537,7 @@
     )(core[None], latent.reshape(n_dev, 2, half, rank), kv)
 
 
-def finish_kernel(x_ref, low_ref, g_ref, dkv_ref, kr_ref, copy_ref, low_t):
+def finish_kernel(x_ref, low_ref, g_ref, up_ref, dkv_ref, kr_ref, copy_ref, uk_ref, uv_ref, low_t):
     @pl.when(pl.program_id(0) == 0)
     def _():
         n_dev, _, shard = low_ref.shape
@@ -549,23 +549,27 @@
     dkv_ref[...] = g[:rank].T
     kr_ref[...] = g[rank:]
     copy_ref[...] = g_ref[...]
-
-
-def finish(x, low, g, rank):
+    spread_heads_kernel(up_ref, uk_ref, uv_ref)
+
+
+def finish(x, low, g, up, rank, nope):
     seq, d_model = x.shape
     width = low.shape[1]
     rope = width - rank
     steps = 4
     cols = d_model // steps
     piece = rows(g.shape[0] // steps, g.shape[1])
+    heads, _, count, width_up = up.shape
+    head_rows = pl.BlockSpec((rank // steps, heads, nope), lambda i: (i, 0, 0))
     return pl.pallas_call(
         finish_kernel, grid=(steps,),
-        in_specs=[pl.BlockSpec((seq, cols), lambda i: (0, i)), whole(*low.shape), piece],
-        out_specs=[rows(cols, rank), pl.BlockSpec((rope, cols), lambda i: (0, i)), piece],
-        out_shape=[struct((d_model, rank)), struct((rope, d_model)), struct(g.shape)],
+        in_specs=[pl.BlockSpec((seq, cols), lambda i: (0, i)), whole(*low.shape), piece,
+                  pl.BlockSpec((heads, 1, count, width_up // 2), lambda i: (0, i // 2, 0, i % 2))],
+        out_specs=[rows(cols, rank), pl.BlockSpec((rope, cols), lambda i: (0, i)), piece, head_rows, head_rows],
+        out_shape=[struct((d_model, rank)), struct((rope, d_model)), struct(g.shape)] + [struct((rank, heads, nope))] * 2,
         scratch_shapes=[pltpu.VMEM((width, seq), BF16)],
         compiler_params=compiler_params(), cost_estimate=cost(2 * x.size * width, 2 * x.size + 8 * g.size),
-    )(x, low, g)
+    )(x, low, g, up)
 
 
 def spread_heads_kernel(up_ref, uk_ref, uv_ref):
@@ -573,17 +577,6 @@
     for a, block in enumerate(jnp.split(up_ref[...].reshape(heads, count, cols), cols // SLOT, axis=2)):
         for ref, value in zip((uk_ref, uv_ref), jnp.split(block, 2, axis=2)):
             ref[a * count:(a + 1) * count] = jnp.swapaxes(value, 0, 1)
-
-
-def spread_heads(up, rank, width):
-    heads, _, count, cols = up.shape
-    steps = 2
-    return pl.pallas_call(
-        spread_heads_kernel, grid=(2, steps),
-        in_specs=[pl.BlockSpec((heads, 1, count, cols // steps), lambda s, a: (0, s, 0, a))],
-        out_specs=[pl.BlockSpec((rank // (2 * steps), heads, width), lambda s, a: (s * steps + a, 0, 0))] * 2,
-        out_shape=[struct((rank, heads, width))] * 2, compiler_params=compiler_params(), cost_estimate=cost(1e9, 8 * up.size),
-    )(up)
 
 
 def solution(mesh):
@@ -637,11 +630,11 @@
         gwo = gather(o_my)
         got_odq, kv_my, _ = lax.optimization_barrier((got_odq, kv_my, o_keep))
         got_kv = exchange(kv_my.reshape(n_dev, half, -1))
+        dkr_my = lax.optimization_barrier((dkr_my, o_my))[0]
+        got_r, = ring_gather(n_dev, 2, [], [dkr_my])
+        got_odq, got_r, kv_my = lax.optimization_barrier((got_odq, got_r, kv_my))
         up_keep, up_give = up_grads(core, latent, kv_my, d_model, n_dev, half)
         up_my = summed(up_keep, up_give)
-        dkr_my, _, _ = lax.optimization_barrier((dkr_my, o_my, up_my))
-        got_r, = ring_gather(n_dev, 2, [], [dkr_my])
-        got_odq, got_r = lax.optimization_barrier((got_odq, got_r))
         o_loc, dq_loc, dq_rope = jnp.split(got_odq, [half, 2 * half], axis=2)
         dq_loc = jnp.concatenate([dq_loc, jnp.concatenate([dq_rope[..., :rope], dq_rope[..., rope:]], axis=2)], axis=3)
         o_loc, dq_loc = o_loc.reshape(heads, shard, -1), dq_loc.reshape(heads, shard, -1)
@@ -666,9 +659,8 @@
         low_my = jnp.concatenate([dc_loc, dkr_raw], axis=1).T
         low_my, dx_loc = lax.optimization_barrier((low_my, dx_loc.astype(BF16)))
         low, up, gg = ring_gather(n_dev, 3, [low_my, up_my], (), [gg_part])
-        gw_dkv, gw_kr, gwq = finish(x_all, low, gwq, rank)
+        gw_dkv, gw_kr, gwq, gw_uk, gw_uv = finish(x_all, low, gwq, up.reshape(heads, 2, -1, d_model), rank, nope)
         gg_kv = jnp.sum(gg, axis=0)[:gg_rows].reshape(rank)
-        gw_uk, gw_uv = spread_heads(up.reshape(heads, 2, -1, d_model), rank, nope)
         gw_q = gwq.reshape(heads, qk_dim, d_model).transpose(2, 0, 1)
         return y_loc, dx_loc, gw_q, gw_dkv, gg_kv, gw_kr.T, gw_uk, gw_uv, gwo.reshape(heads, v_dim, d_model)
 

time: 379 us -> 367 us (0.968)
  Pallas kernels: 275 us -> 269 us
    pallas_call x1 -> x0, Pallas kernels: 7.57 us -> none  [spread_heads(): pl.pallas_call(spread_heads_kernel, grid=(2, steps), in_specs=[pl.BlockSp...]
    pallas_call x1, Pallas kernels: 28 us -> 32.6 us  [finish(): pl.pallas_call(finish_kernel, grid=(steps,), in_specs=[pl.BlockSpec((seq,...]
    pallas_call x3, Pallas kernels: 172 us -> 168 us  [ring_gather(): pl.pallas_call(functools.partial(ring_kernel, side, counts, make, len(giv...]
    dot_general x1, matrix products: 5.92 us -> 2.05 us  [block(): jnp.einsum('htv,hvd->td', o_loc, w_o, preferred_element_type=F32)]
    unnamed x23 -> x25, local copies, waits for them, and re-layouts: 13.6 us -> 12.1 us
where the time goes in v6:
time: 367 us; the launch traced here: 366 us
  Pallas kernels  269 us (73%)
  waiting for transfers between devices  27 us (7%)
  local copies, waits for them, and re-layouts  17.7 us (5%)
  matrix products  16.2 us (4%)
  between operations  14.1 us (4%)
  other arithmetic  13 us (4%)
  starting transfers between devices  9.39 us (3%)
    pallas_call x3, Pallas kernels, ring_gather(): pl.pallas_call(functools.partial(ring_kernel, side, counts, make, len(giv...  168 us
    pallas_call x1, Pallas kernels, attention(): pl.pallas_call(functools.partial(attn_kernel, scale, shard, half, nope, r...  50.9 us
    pallas_call x1, Pallas kernels, finish(): pl.pallas_call(finish_kernel, grid=(steps,), in_specs=[pl.BlockSpec((seq,...  32.6 us
    all_to_all x2, waiting for transfers between devices, exchange(): lax.all_to_all(a, 'cp', 0, 0, tiled=True).reshape(heads, 2, *a.shape[1:])  19.4 us
    pallas_call x2, Pallas kernels, head_grads(): pl.pallas_call(kernel, grid_spec=pltpu.PrefetchScalarGridSpec(num_scalar_...  13.4 us
    unnamed x25, local copies, waits for them, and re-layouts  12.1 us
    all_to_all x2, starting transfers between devices, exchange(): lax.all_to_all(a, 'cp', 0, 0, tiled=True).reshape(heads, 2, *a.shape[1:])  8.3 us
    add x4, other arithmetic, summed(): return keep + lax.ppermute(give, 'cp', siblings)  8.28 us
  transfers between devices with their start and end apart: 9, of which 5 were waited for; matrix products, arithmetic and copies ran while one was open for 10% of the time, Pallas kernels for 56%

profile of v6, /device:TPU:97, one launch (start us, length us, event | category | flops | bytes accessed | tf_op | source)
XLA Modules:
  0.0 365.9 jit_solution(10178017108543354658)
XLA Ops:
  7.3 63.6 %shard_map.178 = (bf16[32,128,2048]{2,1,0:T(8,128)(2,1)}, bf16[32,64,128]{2,1,0:T(8,128)(2,1)}, bf16[512,128]{1,0:T(8,128)(2,1)}, bf16[512,128]{1,0:T(8,128)(2,1)}) custom-call(bf16[128,2048]{1,0:T(8,128)(2,1)} %refs_0_.1, bf16[16,128,2048]{2,1,0:T(8,128)(2,1)} %refs_1_.1, bf16[512,16,128]{2,1,0:T(8,128)(2,1)} %refs_2_.1, bf16[512,16,128]{2,1,0:T(8,128)(2,1)} %refs_3_.1, ...), custom_call_target="tpu_custom_call" | custom-call | flops 40000000000 | tf_op jit(solution)/shard_map/pallas_call | solution.py:413
  72.2 50.9 %shard_map.179 = (bf16[2048,384]{1,0:T(8,128)(2,1)}, bf16[32,160,128]{2,1,0:T(8,128)(2,1)}, f32[2048,384]{1,0:T(8,128)}, f32[2048,384]{1,0:T(8,128)}, bf16[4096,512]{1,0:T(8,128)(2,1)}) custom-call(s32[2]{0:T(128)} %pad_add_fusion.place_ref, bf16[4096,2048]{1,0:T(8,128)(2,1)} %bitcast.48, f32[8,128]{1,0:T(8,128)} %constant.51.clone.far_ref, ...), custom_call_target="tpu_custom_call" | custom-call | flops 27917287424 | bytes 16777216 | tf_op jit(solution)/shard_map/pallas_call | solution.py:233
  123.1 7.2 %shard_map.180 = (f32[96,2048]{1,0:T(8,128)}, f32[96,2048]{1,0:T(8,128)}) custom-call(s32[1]{0:T(128)} %bitcast.core_ref, bf16[32,2,64,2048]{3,2,1,0:T(8,128)(2,1)} %bitcast.49, bf16[2048,384]{1,0:T(8,128)(2,1)} %get-tuple-element.52.odq_ref), custom_call_target="tpu_custom_call" | custom-call | flops 1610612736 | bytes 8388608 | tf_op jit(solution)/shard_map/pallas_call | solution.py:505
  130.4 2.8 collective-permute-done.3
  133.1 2.1 add.64
  135.4 2.1 all-gather.4.cloned.1.call-done
  137.5 6.2 %shard_map.181 = (f32[64,2048]{1,0:T(8,128)}, f32[64,2048]{1,0:T(8,128)}) custom-call(s32[1]{0:T(128)} %bitcast.core_ref, bf16[32,2,64,2048]{3,2,1,0:T(8,128)(2,1)} %bitcast.54, bf16[2048,384]{1,0:T(8,128)(2,1)} %get-tuple-element.52.odq_ref), custom_call_target="tpu_custom_call" | custom-call | flops 1073741824 | bytes 8388608 | tf_op jit(solution)/shard_map/pallas_call | solution.py:505
  143.9 1.9 collective-permute-done.1
  145.8 2.1 add.54
  148.3 4.2 %all-to-all-start = ((bf16[32,160,128]{2,1,0:T(8,128)(2,1)}), bf16[32,160,128]{2,1,0:T(8,128)(2,1)}, u32[]{:S(2)}, u32[]{:S(2)}) async-start(bf16[32,160,128]{2,1,0:T(8,128)(2,1)} %get-tuple-element.54), calls=%async_computation | async-start | bytes 2621440 | tf_op jit(solution)/shard_map/all_to_all | solution.py:618
  154.1 3.3 add.53
  159.8 19.4 %all-to-all-done = bf16[32,160,128]{2,1,0:T(8,128)(2,1)} async-done(((bf16[32,160,128]{2,1,0:T(8,128)(2,1)}), bf16[32,160,128]{2,1,0:T(8,128)(2,1)}, u32[]{:S(2)}, u32[]{:S(2)}) %all-to-all-start) | async-done | bytes 1310752 | tf_op jit(solution)/shard_map/all_to_all | solution.py:618
  179.1 4.1 %all-to-all-start.1 = ((bf16[32,64,256]{2,1,0:T(8,128)(2,1)}), bf16[32,64,256]{2,1,0:T(8,128)(2,1)}, u32[]{:S(2)}, u32[]{:S(2)}) async-start(bf16[32,64,256]{2,1,0:T(8,128)(2,1)} %bitcast.10), calls=%async_computation.1 | async-start | bytes 2097152 | tf_op jit(solution)/shard_map/all_to_all | solution.py:618
  183.2 42.5 %shard_map.182 = f32[32,32,128]{2,1,0:T(8,128)} custom-call(f32[32,32,128]{2,1,0:T(8,128)} %reshape.99.refs_0_), custom_call_target="tpu_custom_call" | custom-call | flops 40000000000 | tf_op jit(solution)/shard_map/pallas_call | solution.py:413
  225.7 3.5 shard_map.183
  229.5 1.3 fusion.31
  230.8 1.5 fusion.30
  232.6 7.1 %convolution_bitcast_fusion.1 = f32[128,2048]{1,0:T(8,128)S(1)} fusion(bf16[16,128,192]{2,1,0:T(8,128)(2,1)S(1)} %bitcast.58, bf16[2048,16,192]{0,2,1:T(8,128)(2,1)} %param.13), kind=kOutput, calls=%fused_computation.3 | convolution fusion | flops 1610612736 | bytes 14417920 | tf_op jit(solution)/shard_map/hte,dhe->td/dot_general | solution.py:642
  239.8 2.1 fusion
  243.1 2.6 fusion.6
  245.8 2.0 multiply_reduce_fusion
  251.4 62.0 %shard_map.184 = (bf16[32,576,128]{2,1,0:T(8,128)(2,1)}, f32[32,32,2048]{2,1,0:T(8,128)}, f32[32,8,128]{2,1,0:T(8,128)}) custom-call(bf16[576,128]{1,0:T(8,128)(2,1)} %maximum_bitcast_fusion.refs_0_, f32[32,2048]{1,0:T(8,128)} %add.63.refs_1_, f32[8,128]{1,0:T(8,128)} %pad.4.refs_2_), custom_call_target="tpu_custom_call" | custom-call | flops 40000000000 | tf_op jit(solution)/shard_map/pallas_call | solution.py:413
  315.0 32.6 %shard_map.185 = (f32[2048,512]{1,0:T(8,128)}, f32[64,2048]{1,0:T(8,128)}, f32[3072,2048]{1,0:T(8,128)}, f32[512,16,128]{2,1,0:T(8,128)}, f32[512,16,128]{2,1,0:T(8,128)}) custom-call(bf16[4096,2048]{1,0:T(8,128)(2,1)} %bitcast.50, bf16[32,576,128]{2,1,0:T(8,128)(2,1)} %get-tuple-element.76.low_ref, f32[3072,2048]{1,0:T(8,128)} %all-gather.6.cloned.1.call-done.g_ref, ...), custom_call_target="tpu_custom_call" | custom-call | flops 9663676416 | bytes 67108864 | tf_op jit(solution)/shard_map/pallas_call | solution.py:564
  347.6 11.8 %copy.60 = f32[16,128,2048]{2,1,0:T(8,128)} copy(f32[16,128,2048]{2,1,0:T(8,128)} %bitcast.53) | data formatting | bytes 33554432
  (66 shorter events, 12.9 us)
Async XLA Ops:
  7.2 63.9 %copy-start.7 = (bf16[512]{0:T(512)(128)(2,1)S(1)}, bf16[512]{0:T(512)(128)(2,1)}, u32[]{:S(2)}) copy-start(bf16[512]{0:T(512)(128)(2,1)} %param.15) | copy-start | bytes 3076
  7.2 130.3 %all-gather.4.cloned.1.call-start = ((), (), s32[]{:S(2)}) async-start(), calls=%async_computation.2 | async-start | bytes 17301504 | tf_op jit(solution)/shard_map/all_gather | solution.py:597
  71.0 244.1 %all-gather.6.cloned.1.call-start = ((), (), s32[]{:S(2)}) async-start(), calls=%async_computation.3 | async-start | bytes 25952256 | tf_op jit(solution)/shard_map/all_gather | solution.py:597
  130.4 2.8 collective-permute-start.3
  135.3 212.3 %all-gather.8.cloned.1.call-start = ((), (), s32[]{:S(2)}) async-start(), calls=%async_computation.4 | async-start | bytes 17301504 | tf_op jit(solution)/shard_map/all_gather | solution.py:597
  143.7 2.1 collective-permute-start.1
  145.8 6.8 %copy-start = (bf16[2048,512]{1,0:T(8,128)(2,1)S(1)}, bf16[2048,512]{1,0:T(8,128)(2,1)}, u32[]{:S(2)}) copy-start(bf16[2048,512]{1,0:T(8,128)(2,1)} %w_ref.1) | copy-start | bytes 6291460
  145.8 6.8 %copy-start.3 = (bf16[128,2048]{1,0:T(8,128)(2,1)S(1)}, bf16[128,2048]{1,0:T(8,128)(2,1)}, u32[]{:S(2)}) copy-start(bf16[128,2048]{1,0:T(8,128)(2,1)} %refs_4_.1) | copy-start | bytes 1572868
  148.0 6.1 %collective-permute-start = (f32[2048,384]{1,0:T(8,128)}, f32[2048,384]{1,0:T(8,128)}, u32[]{:S(2)}, u32[]{:S(2)}) collective-permute-start(f32[2048,384]{1,0:T(8,128)} %get-tuple-element.56), channel_id=1, source_target_pairs={{0,1},{1,0},{2,3},{3,2},{4,5},{5,4},{6,7},{7,6},{8,9},{9,8},{10,11... | collective-permute-start | bytes 9437192 | tf_op jit(solution)/shard_map/ppermute | solution.py:600
  148.3 30.8 %all-to-all-start = ((bf16[32,160,128]{2,1,0:T(8,128)(2,1)}), bf16[32,160,128]{2,1,0:T(8,128)(2,1)}, u32[]{:S(2)}, u32[]{:S(2)}) async-start(bf16[32,160,128]{2,1,0:T(8,128)(2,1)} %get-tuple-element.54), calls=%async_computation | async-start | bytes 2621440 | tf_op jit(solution)/shard_map/all_to_all | solution.py:618
  179.1 63.4 %all-to-all-start.1 = ((bf16[32,64,256]{2,1,0:T(8,128)(2,1)}), bf16[32,64,256]{2,1,0:T(8,128)(2,1)}, u32[]{:S(2)}, u32[]{:S(2)}) async-start(bf16[32,64,256]{2,1,0:T(8,128)(2,1)} %bitcast.10), calls=%async_computation.1 | async-start | bytes 2097152 | tf_op jit(solution)/shard_map/all_to_all | solution.py:618
  229.2 12.6 %collective-permute-start.2 = (f32[32,2048]{1,0:T(8,128)}, f32[32,2048]{1,0:T(8,128)S(1)}, u32[]{:S(2)}, u32[]{:S(2)}) collective-permute-start(f32[32,2048]{1,0:T(8,128)} %get-tuple-element.75), channel_id=1, source_target_pairs={{0,1},{1,0},{2,3},{3,2},{4,5},{5,4},{6,7},{7,6},{8,9},{9,8},{10,11... | collective-permute-start | bytes 786440 | tf_op jit(solution)/shard_map/ppermute | solution.py:600
  229.5 10.3 %slice-start = ((s8[8388608]{0:T(1024)(128)(4,1)}), s8[4194304]{0:T(1024)(128)(4,1)S(1)}, s32[]{:S(2)}) async-start(s8[8388608]{0:T(1024)(128)(4,1)} %bitcast.51), calls=%async_computation.5 | async-start | bytes 8388608
  232.6 7.1 %slice-start.1 = ((s8[8388608]{0:T(1024)(128)(4,1)}), s8[4194304]{0:T(1024)(128)(4,1)S(1)}, s32[]{:S(2)}) async-start(s8[8388608]{0:T(1024)(128)(4,1)} %bitcast.51), calls=%async_computation.6 | async-start | bytes 8388608
  239.8 2.1 copy-start.5
  239.8 2.8 copy-start.2
  242.9 2.9 copy-start.6
  243.1 2.7 copy-start.8
  245.8 3.0 copy-start.1
  248.8 1.0 copy-start.4
Sparse Core Ops, SparseCore 0:
  71.1 66.3 all-gather.3
  139.5 117.6 all-gather.5
  259.9 77.2 all-gather.7
